TPU v7x, 128 devices: a whole 4x4x4 slice. The times are simulated.
128 devices in a mesh: dp: 64 (over z, y, x), mp: 2 (over core).
Axes of the slice: x: 4, y: 4, z: 4, core: 2. Of those that a mesh axis runs over, the one named last changes fastest.
Arguments:
- patches: bfloat16 [32768, 3200], P(('dp', 'mp')), may hold values from -120 to 120
- ln_gain: bfloat16 [3200], replicated, may hold values from 0.099609375 to 1.8984375
- ln_bias: bfloat16 [3200], replicated, may hold values from -3 to 3
- w_proj: bfloat16 [3200, 4096], P(None, 'mp'), may hold values from -0.109375 to 0.109375
- proj_bias: bfloat16 [4096], P('mp'), may hold values from -3 to 3
- rms_gain: bfloat16 [4096], replicated, may hold values from 0.099609375 to 1.8984375
- w_qkv: bfloat16 [4096, 3072], P(None, 'mp'), may hold values from -4 to 4
- image_counts: int32 [256, 8], replicated, may hold values from 1 to 16, as said below
- source_shift: int32 [32], replicated, may hold values from 0 to 63, as said below
Outputs:
- attended: bfloat16 [32768, 2048], P('dp', 'mp')
Inputs may be any that keep to these rules, and one draw needn't show every extreme that they name: `image_counts`: row g holds the counts of the 8 images of tile g. In every draw all images of the tiles of some dp index hold 16 tokens. No value stands more than 1 times in source_shift, and some value stands exactly 1 times.
All inputs are finite; a program needn't handle non-finite values.
Results may differ from a plain program's by a relative error of at most 0.012.
Values may be sent and summed in bfloat16 or wider, within the bound.
No kernel may reach another device: no remote copies, remote signals or barrier semaphores. Data moves between devices by JAX's collectives and lax.ppermute only.
A program may use at most 128 MiB of HBM per device.

v0:
```python
import jax
import jax.numpy as jnp
from jax import lax
from jax.sharding import PartitionSpec as P

HEAD_SIZE = 128
TILE = 128
QUERY_PER_KEY = 4


norm_epsilon = 1e-05
rms_epsilon = 1e-05
rotary_base = 500000.0


def from_everyone(value, axis):
    copies = jnp.broadcast_to(value, (lax.axis_size(axis), *value.shape))
    return lax.all_to_all(copies, axis, split_axis=0, concat_axis=0, tiled=True)


def joined_along(pieces, dim):
    pieces = jnp.moveaxis(pieces, 0, dim)
    lengths = pieces.shape
    return pieces.reshape(*lengths[:dim], lengths[dim] * lengths[dim + 1], *lengths[dim + 2 :])


def collect(value, axis, dim):
    pieces = from_everyone(value, axis)
    return joined_along(pieces, dim)


def layer_norm(row_block, gain_vec, bias_vec):
    values = row_block.astype(jnp.float32)
    row_mean = jnp.mean(values, axis=-1, keepdims=True)
    centred = values - row_mean
    row_var = jnp.mean(centred * centred, axis=-1, keepdims=True)
    scaled = centred * lax.rsqrt(row_var + norm_epsilon) * gain_vec.astype(jnp.float32)
    return (scaled + bias_vec.astype(jnp.float32)).astype(jnp.bfloat16)


def rotary(values, cos_table, sine_table):
    half_width = values.shape[-1] // 2
    turned = jnp.concatenate([-values[..., half_width:], values[..., :half_width]], axis=-1)
    return values * cos_table + turned * sine_table


def attend(queries, key_rows, value_rows, segment):
    tile_count = queries.shape[0] // TILE
    groups = queries.shape[1]
    query_f = queries.reshape(tile_count, TILE, groups, QUERY_PER_KEY, HEAD_SIZE).astype(
        jnp.float32
    )
    key_f = key_rows.reshape(tile_count, TILE, groups, HEAD_SIZE).astype(jnp.float32)
    value_f = value_rows.reshape(tile_count, TILE, groups, HEAD_SIZE).astype(jnp.float32)
    scores = jnp.einsum("tqhgd,tkhd->thgqk", query_f, key_f) * HEAD_SIZE ** (-0.5)
    segments = segment.reshape(tile_count, TILE)
    position = jnp.arange(TILE, dtype=jnp.int32)
    allowed = (position[None, :, None] >= position[None, None, :]) & (
        segments[:, :, None] == segments[:, None, :]
    )
    scores = jnp.where(allowed[:, None, None], scores, -1e30)
    row_max = jnp.max(scores, axis=-1, keepdims=True)
    weights = jnp.exp(scores - row_max)
    probabilities = (weights / jnp.sum(weights, axis=-1, keepdims=True)).astype(jnp.bfloat16)
    attended = jnp.einsum("thgqk,tkhd->tqhgd", probabilities.astype(jnp.float32), value_f)
    return attended.reshape(tile_count * TILE, groups * QUERY_PER_KEY * HEAD_SIZE)


def finish(hidden, live_flat, segment, rms_gain, w_qkv):
    row_total = hidden.shape[0]
    widened = hidden.astype(jnp.float32)
    mean_square = jnp.mean(widened * widened, axis=-1, keepdims=True)
    rms_normed = (
        widened * lax.rsqrt(mean_square + rms_epsilon) * rms_gain.astype(jnp.float32)
    ).astype(jnp.bfloat16)
    projections = jnp.dot(rms_normed, w_qkv, preferred_element_type=jnp.float32)
    groups = w_qkv.shape[1] // ((QUERY_PER_KEY + 2) * HEAD_SIZE)
    projections = projections.reshape(row_total, groups, QUERY_PER_KEY + 2, HEAD_SIZE)
    position = (jnp.arange(row_total, dtype=jnp.int32) % TILE).astype(jnp.float32)
    frequency = rotary_base ** (
        -(jnp.arange(HEAD_SIZE // 2, dtype=jnp.float32) * (2.0 / HEAD_SIZE))
    )
    angles = position[:, None] * frequency[None, :]
    cos_table = jnp.concatenate([jnp.cos(angles), jnp.cos(angles)], axis=-1)[:, None, None, :]
    sine_table = jnp.concatenate([jnp.sin(angles), jnp.sin(angles)], axis=-1)[:, None, None, :]
    queries = rotary(projections[:, :, :QUERY_PER_KEY], cos_table, sine_table).astype(jnp.bfloat16)
    key_rows = rotary(
        projections[:, :, QUERY_PER_KEY], cos_table[:, :, 0], sine_table[:, :, 0]
    ).astype(jnp.bfloat16)
    value_rows = projections[:, :, QUERY_PER_KEY + 1].astype(jnp.bfloat16)
    attended = attend(queries, key_rows, value_rows, segment).astype(jnp.bfloat16)
    return jnp.where(live_flat[:, None], attended, jnp.zeros_like(attended))


def deliver(blocks, source_shift, senders, my_index):
    img_dev = blocks.shape[0]
    img_most = blocks.shape[1]
    images = jnp.arange(img_dev, dtype=jnp.int32)
    pair_slots = (img_dev + senders - 1) // senders
    same_shift = (source_shift[:, None] == source_shift[None, :]) & (
        images[None, :] < images[:, None]
    )
    slot_rank = jnp.sum(same_shift.astype(jnp.int32), axis=1)
    targets = jnp.mod(my_index - source_shift, senders)
    outbox = jnp.zeros((senders * pair_slots, img_most, blocks.shape[2]), jnp.bfloat16)
    outbox = outbox.at[targets * pair_slots + slot_rank].set(blocks)
    in_box = lax.all_to_all(outbox, "dp", split_axis=0, concat_axis=0, tiled=True)
    anchors = jnp.mod(my_index + source_shift, senders)
    arrived = jnp.take(in_box, anchors * pair_slots + slot_rank, axis=0)
    return arrived


def local(
    patches, ln_gain, ln_bias, w_proj, proj_bias, rms_gain, w_qkv, image_counts, source_shift
):
    senders = lax.axis_size("dp")
    my_index = lax.axis_index("dp")
    normed_half = layer_norm(patches, ln_gain, ln_bias)
    normed = collect(normed_half, "mp", 0)
    tok_rows = normed.shape[0]
    pre_act = jnp.dot(normed, w_proj, preferred_element_type=jnp.float32) + proj_bias.astype(
        jnp.float32
    )
    projected = jax.nn.gelu(pre_act, approximate=False).astype(jnp.bfloat16)
    img_dev = source_shift.shape[0]
    tiles_dev = tok_rows // TILE
    img_tile = img_dev // tiles_dev
    img_most = TILE // img_tile
    per_dest = image_counts.reshape(senders, img_dev)
    images = jnp.arange(img_dev, dtype=jnp.int32)
    targets = jnp.mod(my_index - source_shift, senders)
    sent_counts = per_dest[targets, images]
    starts = jnp.cumsum(sent_counts) - sent_counts
    inside = jnp.arange(img_most, dtype=jnp.int32)
    pick_rows = jnp.minimum(starts[:, None] + inside[None, :], tok_rows - 1).reshape(-1)
    blocks = jnp.take(projected, pick_rows, axis=0).reshape(img_dev, img_most, projected.shape[1])
    arrived = deliver(blocks, source_shift, senders, my_index)
    my_tiles = lax.dynamic_slice_in_dim(image_counts, my_index * tiles_dev, tiles_dev, 0)
    slot_ends = jnp.cumsum(my_tiles, axis=1)
    offsets = slot_ends - my_tiles
    position = jnp.arange(TILE, dtype=jnp.int32)
    slot_index = jnp.sum(
        (position[None, :, None] >= slot_ends[:, None, :]).astype(jnp.int32), axis=2
    )
    live_rows = slot_index < img_tile
    clipped = jnp.minimum(slot_index, img_tile - 1)
    inside_tile = position[None, :] - jnp.take_along_axis(offsets, clipped, axis=1)
    image_k = jnp.arange(tiles_dev, dtype=jnp.int32)[:, None] * img_tile + clipped
    pick_back = jnp.where(live_rows, image_k * img_most + inside_tile, 0).reshape(-1)
    placed = jnp.take(arrived.reshape(img_dev * img_most, arrived.shape[2]), pick_back, axis=0)
    live_flat = live_rows.reshape(-1)
    hidden_half = jnp.where(live_flat[:, None], placed, jnp.zeros_like(placed))
    hidden = collect(hidden_half, "mp", 1)
    return finish(hidden, live_flat, slot_index.reshape(-1), rms_gain, w_qkv)


def solution(mesh):
    in_specs = (
        P(("dp", "mp"), None),
        P(),
        P(),
        P(None, "mp"),
        P("mp"),
        P(),
        P(None, "mp"),
        P(),
        P(),
    )
    out_specs = P("dp", "mp")
    return jax.shard_map(local, mesh=mesh, in_specs=in_specs, out_specs=out_specs, check_vma=False)
```

profile of v0, /device:TPU:0, one launch (start us, length us, event | category | flops | bytes accessed | tf_op | source)
XLA Modules:
  0.0 184.9 jit_solution(15312246587526553117)
XLA Ops:
  0.0 1.9 %convert_reduce_fusion = f32[256]{0:T(256)S(1)} fusion(bf16[256,3200]{1,0:T(8,128)(2,1)} %param.11), kind=kLoop, calls=%fused_computation.32 | loop fusion | flops 1638144 | bytes 1639424 | tf_op jit(solution)/shard_map/reduce_sum | solution.py:34
  1.9 2.0 %fusion.16 = f32[256]{0:T(256)S(1)} fusion(bf16[256,3200]{1,0:T(8,128)(2,1)} %param.11, f32[256]{0:T(256)S(1)} %broadcast_multiply_fusion), kind=kLoop, calls=%fused_computation.35 | loop fusion | flops 3276544 | bytes 1640448 | tf_op jit(solution)/shard_map/reduce_sum | solution.py:36
  3.9 0.7 convert_element_type.93
  4.6 0.7 convert_element_type.94
  5.3 0.8 fusion.19
  6.1 1.9 %broadcast_in_dim.114 = bf16[2,256,3200]{2,1,0:T(8,128)(2,1)} broadcast(bf16[256,3200]{1,0:T(8,128)(2,1)S(1)} %fusion.19), dimensions={1,2} | broadcast | bytes 4915200 | tf_op jit(solution)/shard_map/broadcast_in_dim | solution.py:17
  8.0 4.1 %all-to-all-start = ((bf16[2,256,3200]{2,1,0:T(8,128)(2,1)}), bf16[2,256,3200]{2,1,0:T(8,128)(2,1)S(1)}, u32[]{:S(2)}, u32[]{:S(2)}) async-start(bf16[2,256,3200]{2,1,0:T(8,128)(2,1)} %broadcast_in_dim.114), calls=%async_computation | async-start | bytes 6553600 | tf_op jit(solution)/shard_map/all_to_all | solution.py:18
  12.2 0.1 copy.55
  12.3 0.1 reshape.232
  12.4 0.7 gather_fusion
  13.1 0.1 copy.56
  13.3 0.1 reduce.2
  13.5 0.1 min.37
  13.6 0.2 convert_reduce_fusion.1
  13.8 2.0 %all-to-all-done = bf16[2,256,3200]{2,1,0:T(8,128)(2,1)S(1)} async-done(((bf16[2,256,3200]{2,1,0:T(8,128)(2,1)}), bf16[2,256,3200]{2,1,0:T(8,128)(2,1)S(1)}, u32[]{:S(2)}, u32[]{:S(2)}) %all-to-all-start) | async-done | bytes 3276832 | tf_op jit(solution)/shard_map/all_to_all | solution.py:18
  15.8 1.7 copy-done.3
  17.5 19.8 %fusion.6 = bf16[512,2048]{1,0:T(8,128)(2,1)S(1)} fusion(bf16[512,3200]{1,0:T(8,128)(2,1)} %bitcast.109, bf16[3200,2048]{1,0:T(8,128)(2,1)} %param.14, f32[2048]{0:T(1024)S(1)} %convert_element_type.96), kind=kOutput, calls=%fused_computation.15 | convolution fusion | flops 6780092416 | bytes 18489344 | tf_op jit(solution)/shard_map/dot_general | solution.py:121
  37.3 3.3 %gather_fusion.3 = bf16[512,2048]{1,0:T(8,128)(2,1)} fusion(bf16[512,2048]{1,0:T(8,128)(2,1)S(1)} %fusion.6, s32[1024]{0:T(1024)S(1)} %pad_clamp_fusion.2), kind=kCustom, calls=%fused_computation.clone | custom fusion | bytes 4196352 | tf_op jit(solution)/shard_map/jit(_take)/gather | solution.py:136
  40.7 1.8 broadcast_select_fusion
  42.5 2.4 %broadcast_in_dim.112 = bf16[64,16,2048]{2,1,0:T(8,128)(2,1)} broadcast(bf16[]{:T(256)} %constant.70.clone.1), dimensions={} | broadcast | bytes 4194306 | tf_op jit(solution)/shard_map/broadcast_in_dim | solution.py:105
  45.0 5.4 %scatter_fusion = bf16[64,16,2048]{2,1,0:T(8,128)(2,1)} fusion(bf16[64,16,2048]{2,1,0:T(8,128)(2,1)} %broadcast_in_dim.112, s32[32]{0:T(128)S(1)} %compare_select_fusion.5, bf16[32,16,2048]{2,1,0:T(8,128)(2,1)S(1)} %bitcast.107), kind=kCustom, calls=%fused_computation.5 | custom fusion | bytes 6291584 | tf_op jit(solution)/shard_map/scatter | solution.py:106
  50.4 11.9 %all-to-all-start.1 = ((bf16[64,16,2048]{2,1,0:T(8,128)(2,1)}), bf16[64,16,2048]{2,1,0:T(8,128)(2,1)}, u32[]{:S(2)}, u32[]{:S(2)}) async-start(bf16[64,16,2048]{2,1,0:T(8,128)(2,1)} %scatter_fusion), calls=%async_computation.1 | async-start | bytes 8388608 | tf_op jit(solution)/shard_map/all_to_all | solution.py:107
  62.3 0.1 constant_dynamic-slice_fusion
  62.4 0.1 copy.54
  62.6 0.1 broadcast_in_dim.110
  62.7 16.7 %copy.58 = bf16[4096,1536]{0,1:T(8,128)(2,1)} copy(bf16[4096,1536]{1,0:T(8,128)(2,1)} %param.17) | data formatting | bytes 25165824 | tf_op args[6]
  79.4 0.1 convert_reduce_fusion.2
  79.6 2.6 %gather_fusion.2 = s32[512]{0:T(512)S(1)} fusion(s32[4,8]{0,1:T(8,128)S(1)} %fusion.89, s32[512]{0:T(512)S(1)} %fusion.44), kind=kCustom, calls=%fused_computation.4 | custom fusion | bytes 8192 | tf_op jit(solution)/shard_map/jit(take_along_axis)/gather | solution.py:147
  82.3 0.1 compare_and_fusion.1
  82.4 0.5 multiply_cosine_fusion.1
  82.9 0.8 pad_maximum_fusion.2
  83.7 1.0 multiply_cosine_fusion
  84.7 1.0 pad_maximum_fusion
  85.7 0.1 compare_and_fusion
  85.8 30.8 %all-to-all-done.1 = bf16[64,16,2048]{2,1,0:T(8,128)(2,1)} async-done(((bf16[64,16,2048]{2,1,0:T(8,128)(2,1)}), bf16[64,16,2048]{2,1,0:T(8,128)(2,1)}, u32[]{:S(2)}, u32[]{:S(2)}) %all-to-all-start.1) | async-done | bytes 4194336 | tf_op jit(solution)/shard_map/all_to_all | solution.py:107
  116.7 4.2 %gather_fusion.1 = bf16[32,16,2048]{2,1,0:T(8,128)(2,1)} fusion(bf16[64,16,2048]{2,1,0:T(8,128)(2,1)} %all-to-all-done.1, s32[1024]{0:T(1024)S(1)} %pad_clamp_fusion.1), kind=kCustom, calls=%fused_computation.3 | custom fusion | bytes 4194432 | tf_op jit(solution)/shard_map/jit(_take)/gather | solution.py:109
  120.9 1.8 bitcast_select_fusion.1
  122.7 3.3 %gather_fusion.4 = bf16[512,2048]{1,0:T(8,128)(2,1)} fusion(bf16[512,2048]{1,0:T(8,128)(2,1)S(1)} %bitcast_select_fusion.1, s32[1024]{0:T(1024)S(1)} %pad_clamp_fusion), kind=kCustom, calls=%fused_computation.1.clone | custom fusion | bytes 4196352 | tf_op jit(solution)/shard_map/jit(_take)/gather | solution.py:150
  126.0 1.9 %select_select_fusion = bf16[512,2048]{1,0:T(8,128)(2,1)S(1)} fusion(bf16[512,2048]{1,0:T(8,128)(2,1)} %gather_fusion.4, pred[512]{0:T(512)(128)(4,1)S(1)} %get-tuple-element.6, pred[512]{0:T(512)(128)(4,1)S(1)} %compare_bitcast_fusion), kind=kLoop, calls=%fused_computation.45 | loop fusion | flops 2097152 | bytes 4195328 | tf_op jit(solution)/shard_map/jit(_where)/select_n | solution.py:152
  127.9 0.5 broadcast_in_dim.120
  128.5 8.2 %all_to_all.15 = bf16[2,512,2048]{2,1,0:T(8,128)(2,1)} all-to-all(bf16[2,512,2048]{2,1,0:T(8,128)(2,1)S(1)} %broadcast_in_dim.120), channel_id=1, replica_groups=mesh['dp'=64,'mp'=2] {'mp'}, dimensions={0} | all-to-all | bytes 8388608 | tf_op jit(solution)/shard_map/all_to_all | solution.py:18
  136.7 6.2 %copy.57 = bf16[2,512,2048]{1,2,0:T(8,128)(2,1)} copy(bf16[2,512,2048]{2,1,0:T(8,128)(2,1)} %all_to_all.15) | data formatting | bytes 8388608 | tf_op jit(solution)/shard_map/all_to_all | solution.py:18
  142.9 3.3 %fusion.1 = f32[512]{0:T(512)S(1)} fusion(bf16[2,512,2048]{1,2,0:T(8,128)(2,1)} %copy.57), kind=kLoop, calls=%fused_computation.9 | loop fusion | flops 6290944 | bytes 4196352 | tf_op jit(solution)/shard_map/reduce_sum | solution.py:72
  146.2 0.2 copy-done
  146.3 1.1 fusion.3
  147.4 9.3 %fusion.84 = f32[512,2,6,128]{0,3,2,1:T(8,128)S(1)} fusion(bf16[512,4096,1,1]{0,1,3,2:T(8,128)(2,1)S(1)} %bitcast.108, bf16[2,6,128,4096]{3,2,1,0:T(8,128)(2,1)} %bitcast.106), kind=kOutput, calls=%fused_computation.150 | convolution fusion | flops 6442450944 | bytes 19922944 | tf_op jit(solution)/shard_map/dot_general | solution.py:76
  156.7 1.7 slice_negate_fusion
  158.4 0.9 fusion.78
  159.3 0.7 slice.59
  160.0 0.9 slice_negate_fusion.1
  160.8 1.7 concatenate.28
  162.6 2.0 %copy.61 = f32[4,128,2,64]{3,1,2,0:T(8,128)} copy(f32[4,128,2,64]{1,0,3,2:T(4,128)} %concatenate.28) | data formatting | bytes 524288 | tf_op jit(solution)/shard_map/concatenate | solution.py:43
  164.5 1.7 concatenate.29
  166.3 2.0 %copy.62 = f32[4,128,2,64]{3,1,2,0:T(8,128)} copy(f32[4,128,2,64]{1,0,3,2:T(4,128)} %concatenate.29) | data formatting | bytes 524288 | tf_op jit(solution)/shard_map/concatenate | solution.py:43
  168.2 2.0 %squeeze.6 = f32[4,128,2,128]{1,0,3,2:T(4,128)} reshape(f32[512,2,1,128]{0,3,2,1:T(8,128)} %get-tuple-element.12) | data formatting | bytes 1048576 | tf_op jit(solution)/shard_map/squeeze | solution.py:88
  170.3 2.0 %copy.60 = f32[4,128,2,128]{3,1,2,0:T(8,128)} copy(f32[4,128,2,128]{1,0,3,2:T(4,128)} %squeeze.6) | data formatting | bytes 1048576 | tf_op jit(solution)/shard_map/squeeze | solution.py:88
  172.3 2.3 %fusion.24 = bf16[2,4,16,4,8,128]{5,4,3,2,1,0:T(8,128)(2,1)S(1)} fusion(f32[512,2,4,64]{0,3,2,1:T(8,128)} %get-tuple-element.15, f32[512,2,4,64]{0,3,2,1:T(8,128)} %get-tuple-element.14, f32[512,2,6,128]{0,3,2,1:T(8,128)S(1)} %fusion.84, f32[512,128]{0,1:T(8,128)} %get-tuple-element.23, f32[512,128]{0,1:T(8,128)S(1)} %get-tuple-element.22), kind=kLoop, calls=%fused_computation.52 | loop fusion | flops 2621440 | bytes 5767168
  174.7 0.9 copy-done.2
  175.6 1.9 %fusion.25 = f32[4,2,128,128,4]{3,2,4,1,0:T(8,128)} fusion(bf16[2,4,16,4,8,128]{5,4,3,2,1,0:T(8,128)(2,1)S(1)} %fusion.24, f32[4,128,2,64]{3,1,2,0:T(8,128)S(1)} %copy-done.6, f32[4,128,2,64]{3,1,2,0:T(8,128)S(1)} %copy-done.4, f32[4,128,2,128]{3,1,2,0:T(8,128)S(1)} %copy-done.8, f32[4,128,128]{2,1,0:T(8,128)S(1)} %copy-done.12, ...), kind=kOutput, calls=%fused_computation.53 | convolution fusion | flops 134873088 | bytes 4718592 | tf_op jit(solution)/shard_map/tqhgd,tkhd->thgqk/dot_general | solution.py:55
  177.5 2.2 %fusion.79 = f32[4,2,4,128]{3,2,1,0:T(4,128)S(1)} fusion(pred[4,128,128]{1,2,0:T(8,128)(4,1)S(1)} %compare_and_fusion, bf16[2,4,16,4,8,128]{5,4,3,2,1,0:T(8,128)(2,1)} %copy-done.2, f32[4,128,2,64]{3,1,2,0:T(8,128)S(1)} %copy-done.7, f32[4,128,2,64]{3,1,2,0:T(8,128)S(1)} %copy-done.5, f32[4,128,2,128]{3,1,2,0:T(8,128)S(1)} %copy-done.9, ...), kind=kOutput, calls=%fused_computation.149 | convolution fusion | flops 136970368 | bytes 2703360 | tf_op jit(solution)/shard_map/sub | solution.py:63
  179.8 2.5 %fusion.23 = bf16[4,128,2,4,128]{1,4,3,2,0:T(8,128)(2,1)S(1)} fusion(f32[4,2,4,128]{3,2,1,0:T(4,128)S(1)} %fusion.79, bf16[4,128,2,128,1]{1,0,3,2,4:T(4,128)(2,1)S(1)} %bitcast.110, f32[4,2,128,128,4]{3,2,4,1,0:T(8,128)} %fusion.25, pred[4,128,128]{1,2,0:T(8,128)(4,1)S(1)} %compare_and_fusion), kind=kOutput, calls=%fused_computation.51 | convolution fusion | flops 137367680 | bytes 3489792 | tf_op jit(solution)/shard_map/thgqk,tkhd->tqhgd/dot_general | solution.py:65
  182.3 0.7 copy.66
  183.0 0.8 convert_element_type.110
  183.8 1.1 broadcast_select_fusion.1
  (62 shorter events, 0.6 us)
Async XLA Ops:
  0.0 5.3 %copy-start.1 = (bf16[256,3200]{1,0:T(8,128)(2,1)S(1)}, bf16[256,3200]{1,0:T(8,128)(2,1)}, u32[]{:S(2)}) copy-start(bf16[256,3200]{1,0:T(8,128)(2,1)} %param.11) | copy-start | bytes 4915204
  8.0 4.1 %copy-start.15 = (s32[256,8]{0,1:T(8,128)S(1)}, s32[256,8]{0,1:T(8,128)}, u32[]{:S(2)}) copy-start(s32[256,8]{0,1:T(8,128)} %param.18) | copy-start | bytes 24580
  8.0 4.4 %copy-start.18 = (s32[32]{0:T(128)S(1)}, s32[32]{0:T(128)}, u32[]{:S(2)}) copy-start(s32[32]{0:T(128)} %param.19) | copy-start | bytes 388
  8.0 5.7 %copy-start.17 = (bf16[2048]{0:T(1024)(128)(2,1)S(1)}, bf16[2048]{0:T(1024)(128)(2,1)}, u32[]{:S(2)}) copy-start(bf16[2048]{0:T(1024)(128)(2,1)} %param.15) | copy-start | bytes 12292
  8.0 7.8 %all-to-all-start = ((bf16[2,256,3200]{2,1,0:T(8,128)(2,1)}), bf16[2,256,3200]{2,1,0:T(8,128)(2,1)S(1)}, u32[]{:S(2)}, u32[]{:S(2)}) async-start(bf16[2,256,3200]{2,1,0:T(8,128)(2,1)} %broadcast_in_dim.114), calls=%async_computation | async-start | bytes 6553600 | tf_op jit(solution)/shard_map/all_to_all | solution.py:18
  15.8 1.7 copy-start.3
  50.4 12.3 %copy-start.16 = (bf16[4096]{0:T(1024)(128)(2,1)S(1)}, bf16[4096]{0:T(1024)(128)(2,1)}, u32[]{:S(2)}) copy-start(bf16[4096]{0:T(1024)(128)(2,1)} %param.16) | copy-start | bytes 24580
  50.4 66.3 %all-to-all-start.1 = ((bf16[64,16,2048]{2,1,0:T(8,128)(2,1)}), bf16[64,16,2048]{2,1,0:T(8,128)(2,1)}, u32[]{:S(2)}, u32[]{:S(2)}) async-start(bf16[64,16,2048]{2,1,0:T(8,128)(2,1)} %scatter_fusion), calls=%async_computation.1 | async-start | bytes 8388608 | tf_op jit(solution)/shard_map/all_to_all | solution.py:107
  142.9 3.4 %copy-start = (bf16[2,512,2048]{1,2,0:T(8,128)(2,1)S(1)}, bf16[2,512,2048]{1,2,0:T(8,128)(2,1)}, u32[]{:S(2)}) copy-start(bf16[2,512,2048]{1,2,0:T(8,128)(2,1)} %copy.57) | copy-start | bytes 12582916
  172.3 3.3 %copy-start.4 = (f32[4,128,2,64]{3,1,2,0:T(8,128)S(1)}, f32[4,128,2,64]{3,1,2,0:T(8,128)}, u32[]{:S(2)}) copy-start(f32[4,128,2,64]{3,1,2,0:T(8,128)} %copy.61) | copy-start | bytes 786436
  172.3 3.3 %copy-start.6 = (f32[4,128,2,64]{3,1,2,0:T(8,128)S(1)}, f32[4,128,2,64]{3,1,2,0:T(8,128)}, u32[]{:S(2)}) copy-start(f32[4,128,2,64]{3,1,2,0:T(8,128)} %copy.62) | copy-start | bytes 786436
  172.3 3.3 %copy-start.8 = (f32[4,128,2,128]{3,1,2,0:T(8,128)S(1)}, f32[4,128,2,128]{3,1,2,0:T(8,128)}, u32[]{:S(2)}) copy-start(f32[4,128,2,128]{3,1,2,0:T(8,128)} %copy.60) | copy-start | bytes 1572868
  172.3 3.3 %copy-start.10 = (f32[4,128,128]{2,1,0:T(8,128)S(1)}, f32[4,128,128]{2,1,0:T(8,128)}, u32[]{:S(2)}) copy-start(f32[4,128,128]{2,1,0:T(8,128)} %get-tuple-element.24) | copy-start | bytes 786436
  172.3 3.3 %copy-start.12 = (f32[4,128,128]{2,1,0:T(8,128)S(1)}, f32[4,128,128]{2,1,0:T(8,128)}, u32[]{:S(2)}) copy-start(f32[4,128,128]{2,1,0:T(8,128)} %get-tuple-element.25) | copy-start | bytes 786436
  174.6 1.0 copy-start.2
  174.6 2.9 %copy-start.5 = (f32[4,128,2,64]{3,1,2,0:T(8,128)S(1)}, f32[4,128,2,64]{3,1,2,0:T(8,128)}, u32[]{:S(2)}) copy-start(f32[4,128,2,64]{3,1,2,0:T(8,128)} %copy.61) | copy-start | bytes 786436
  174.6 2.8 %copy-start.7 = (f32[4,128,2,64]{3,1,2,0:T(8,128)S(1)}, f32[4,128,2,64]{3,1,2,0:T(8,128)}, u32[]{:S(2)}) copy-start(f32[4,128,2,64]{3,1,2,0:T(8,128)} %copy.62) | copy-start | bytes 786436
  174.7 2.8 %copy-start.9 = (f32[4,128,2,128]{3,1,2,0:T(8,128)S(1)}, f32[4,128,2,128]{3,1,2,0:T(8,128)}, u32[]{:S(2)}) copy-start(f32[4,128,2,128]{3,1,2,0:T(8,128)} %copy.60) | copy-start | bytes 1572868
  174.7 2.8 %copy-start.11 = (f32[4,128,128]{2,1,0:T(8,128)S(1)}, f32[4,128,128]{2,1,0:T(8,128)}, u32[]{:S(2)}) copy-start(f32[4,128,128]{2,1,0:T(8,128)} %get-tuple-element.24) | copy-start | bytes 786436
  174.7 2.8 %copy-start.13 = (f32[4,128,128]{2,1,0:T(8,128)S(1)}, f32[4,128,128]{2,1,0:T(8,128)}, u32[]{:S(2)}) copy-start(f32[4,128,128]{2,1,0:T(8,128)} %get-tuple-element.25) | copy-start | bytes 786436
  175.6 4.1 %copy-start.14 = (bf16[512,2,1,128]{0,3,2,1:T(8,128)(2,1)S(1)}, bf16[512,2,1,128]{0,3,2,1:T(8,128)(2,1)}, u32[]{:S(2)}) copy-start(bf16[512,2,1,128]{0,3,2,1:T(8,128)(2,1)} %slice.59) | copy-start | bytes 786436
where the time goes:
time: 187 us; the launch traced here: 185 us
  local copies, waits for them, and re-layouts  65.6 us (35%)
  matrix products  35.6 us (19%)
  waiting for transfers between devices  32.9 us (18%)
  other arithmetic  26.2 us (14%)
  starting transfers between devices  16 us (9%)
  blocking collectives  8.18 us (4%)
    all_to_all x1, waiting for transfers between devices, deliver(): lax.all_to_all(outbox, 'dp', split_axis=0, concat_axis=0, tiled=True)  30.8 us
    dot_general x1, matrix products, local(): jnp.dot(normed, w_proj, preferred_element_type=jnp.float32)  19.8 us
    unnamed x40, local copies, waits for them, and re-layouts  19.6 us
    all_to_all x1, starting transfers between devices, deliver(): lax.all_to_all(outbox, 'dp', split_axis=0, concat_axis=0, tiled=True)  11.9 us
    dot_general x1, matrix products, finish(): projections = jnp.dot(rms_normed, w_qkv, preferred_element_type=jnp.float32)  9.31 us
    all_to_all x1, blocking collectives, from_everyone(): return lax.all_to_all(copies, axis, split_axis=0, concat_axis=0, tiled=True)  8.18 us
    concatenate x4, local copies, waits for them, and re-layouts, rotary(): jnp.concatenate([-values[..., half_width:], values[..., :half_width]], ax...  7.4 us
    all_to_all x1, local copies, waits for them, and re-layouts, from_everyone(): return lax.all_to_all(copies, axis, split_axis=0, concat_axis=0, tiled=True)  6.22 us
  transfers between devices with their start and end apart: 2, of which 2 were waited for; matrix products, arithmetic and copies ran while one was open for 14% of the time, Pallas kernels for 0%

commit v1 on v0

v1 whole, which is shorter than its diff:
```python
import functools

import jax
import jax.numpy as jnp
import numpy as np
from jax import lax
from jax.experimental import pallas as pl
from jax.experimental.pallas import tpu as pltpu
from jax.sharding import PartitionSpec as P

HEAD_SIZE = 128
TILE = 128
QUERY_PER_KEY = 4
IMG_MAX = 16

norm_epsilon = 1e-05
rms_epsilon = 1e-05
rotary_base = 500000.0

SWAP = [(0, 1), (1, 0)]
VMEM_BYTES = 56 * 1024 * 1024


def rotary_tables():
    half = HEAD_SIZE // 2
    frequency = rotary_base ** (-(np.arange(half, dtype=np.float64) * (2.0 / HEAD_SIZE)))
    angles = np.arange(IMG_MAX, dtype=np.float64)[:, None] * frequency[None, :]
    cos = np.concatenate([np.cos(angles), np.cos(angles)], axis=-1)
    sine = np.concatenate([-np.sin(angles), np.sin(angles)], axis=-1)
    return cos.astype(np.float32), sine.astype(np.float32)


def normalised(rows, gain, bias):
    values = rows.astype(jnp.float32)
    width = values.shape[-1]
    row_mean = jnp.sum(values, axis=-1, keepdims=True) * (1.0 / width)
    centred = values - row_mean
    row_var = jnp.sum(centred * centred, axis=-1, keepdims=True) * (1.0 / width)
    scaled = centred * lax.rsqrt(row_var + norm_epsilon) * gain.astype(jnp.float32)
    return (scaled + bias.astype(jnp.float32)).astype(jnp.bfloat16)


def norm_body(rows_ref, gain_ref, bias_ref, out_ref):
    out_ref[...] = normalised(rows_ref[...], gain_ref[...], bias_ref[...])


def layer_norm(rows, gain, bias):
    count, width = rows.shape
    step = 32
    return pl.pallas_call(
        norm_body,
        grid=(count // step,),
        in_specs=[
            pl.BlockSpec((step, width), lambda i: (i, 0)),
            pl.BlockSpec((1, width), lambda i: (0, 0)),
            pl.BlockSpec((1, width), lambda i: (0, 0)),
        ],
        out_specs=pl.BlockSpec((step, width), lambda i: (i, 0)),
        out_shape=jax.ShapeDtypeStruct((count, width), jnp.bfloat16),
        cost_estimate=pl.CostEstimate(
            flops=10 * count * width, bytes_accessed=4 * count * width, transcendentals=0
        ),
        name="layer_norm",
    )(rows, gain, bias)


def project_body(
    place_ref, counts_ref, shift_ref, own_ref, other_ref, gain_ref, bias_ref, w_ref, add_ref,
    out_ref, normed, align, acc,
):
    step = pl.program_id(0)
    last = pl.num_programs(0) - 1
    half = own_ref.shape[0]
    rows = 2 * half
    images = shift_ref.shape[0]
    senders = counts_ref.shape[0] // images

    @pl.when(step == 0)
    def _():
        core = place_ref[1]
        normed[pl.ds(pl.multiple_of(core * half, half), half), :] = own_ref[...]
        base = (1 - core) * half
        block = 32

        def fill(i, carry):
            src = pl.multiple_of(i * block, block)
            dst = pl.multiple_of(base + i * block, block)
            normed[pl.ds(dst, block), :] = normalised(
                other_ref[pl.ds(src, block), :], gain_ref[...], bias_ref[...]
            )
            return carry

        lax.fori_loop(0, half // block, fill, 0)
        column = lax.broadcasted_iota(jnp.int32, (IMG_MAX, rows), 1)
        inside = lax.broadcasted_iota(jnp.int32, (IMG_MAX, rows), 0)
        distance = column - inside
        start = jnp.int32(0)
        for k in range(images):
            align[k * IMG_MAX : (k + 1) * IMG_MAX, :] = jnp.where(
                distance == start, 1.0, 0.0
            ).astype(jnp.bfloat16)
            target = lax.rem(place_ref[0] - shift_ref[k] + senders, senders)
            start = start + counts_ref[target * images + k]

    def post():
        slot = lax.rem(step + 1, 2)
        pre = acc[slot] + add_ref[...].astype(jnp.float32)
        value = pre * (1.0 + lax.erf(pre * np.float32(0.5**0.5))) * 0.5
        out_ref[...] = jnp.dot(
            align[...], value.astype(jnp.bfloat16), preferred_element_type=jnp.float32
        ).astype(jnp.bfloat16)

    @pl.when(step < last)
    def _():
        acc[lax.rem(step, 2)] = jnp.dot(
            normed[...], w_ref[...], preferred_element_type=jnp.float32
        )
        post()

    @pl.when(step == last)
    def _():
        post()


def project(place, counts, shift, own, other, gain, bias, w_proj, proj_bias):
    half, width = own.shape
    rows = 2 * half
    columns = w_proj.shape[1]
    block = 256
    steps = columns // block
    whole = lambda j, *_: (0, 0)
    before = lambda j, *_: (0, jnp.maximum(j - 1, 0))
    return pl.pallas_call(
        project_body,
        grid_spec=pltpu.PrefetchScalarGridSpec(
            num_scalar_prefetch=3,
            grid=(steps + 1,),
            in_specs=[
                pl.BlockSpec((half, width), whole),
                pl.BlockSpec((half, width), whole),
                pl.BlockSpec((1, width), whole),
                pl.BlockSpec((1, width), whole),
                pl.BlockSpec((width, block), lambda j, *_: (0, jnp.minimum(j, steps - 1))),
                pl.BlockSpec((1, block), before),
            ],
            out_specs=pl.BlockSpec((rows, block), before),
            scratch_shapes=[
                pltpu.VMEM((rows, width), jnp.bfloat16),
                pltpu.VMEM((rows, rows), jnp.bfloat16),
                pltpu.VMEM((2, rows, block), jnp.float32),
            ],
        ),
        out_shape=jax.ShapeDtypeStruct((rows, columns), jnp.bfloat16),
        compiler_params=pltpu.CompilerParams(vmem_limit_bytes=VMEM_BYTES),
        cost_estimate=pl.CostEstimate(
            flops=2 * rows * width * columns,
            bytes_accessed=2 * width * columns,
            transcendentals=rows * columns,
        ),
        name="project",
    )(place, counts, shift, own, other, gain, bias, w_proj, proj_bias)


def lane_squares(values):
    total = None
    for c in range(values.shape[1] // 128):
        piece = values[:, c * 128 : (c + 1) * 128].astype(jnp.float32)
        total = piece * piece if total is None else total + piece * piece
    return total


def first_half_body(place_ref, hidden_ref, gain_ref, w_ref, part_ref, square_ref, gained):
    @pl.when(pl.program_id(0) == 0)
    def _():
        gained[...] = hidden_ref[...] * gain_ref[...]
        square_ref[...] = lane_squares(hidden_ref[...])

    part_ref[...] = jnp.dot(gained[...], w_ref[...], preferred_element_type=jnp.float32)


def first_half(place, hidden, rms_gain, w_qkv):
    rows, depth = hidden.shape
    columns = w_qkv.shape[1]
    block = 256
    return pl.pallas_call(
        first_half_body,
        grid_spec=pltpu.PrefetchScalarGridSpec(
            num_scalar_prefetch=1,
            grid=(columns // block,),
            in_specs=[
                pl.BlockSpec((rows, depth), lambda j, place: (0, 0)),
                pl.BlockSpec((1, depth), lambda j, place: (0, place[1])),
                pl.BlockSpec((depth, block), lambda j, place: (place[1], j)),
            ],
            out_specs=[
                pl.BlockSpec((rows, block), lambda j, place: (0, j)),
                pl.BlockSpec((rows, 128), lambda j, place: (0, 0)),
            ],
            scratch_shapes=[pltpu.VMEM((rows, depth), jnp.bfloat16)],
        ),
        out_shape=[
            jax.ShapeDtypeStruct((rows, columns), jnp.float32),
            jax.ShapeDtypeStruct((rows, 128), jnp.float32),
        ],
        compiler_params=pltpu.CompilerParams(vmem_limit_bytes=VMEM_BYTES),
        cost_estimate=pl.CostEstimate(
            flops=2 * rows * depth * columns,
            bytes_accessed=2 * depth * columns + 4 * rows * columns,
            transcendentals=0,
        ),
        name="first_half",
    )(place, hidden, rms_gain, w_qkv)


def attend_body(
    place_ref, shift_ref, hidden_ref, gain_ref, w_ref, part_ref, square_ref, cos_ref, sine_ref,
    out_ref, gained, factor, heads,
):
    step = pl.program_id(0)
    rows, depth = hidden_ref.shape
    images = shift_ref.shape[0]
    senders = out_ref.shape[0]
    per_tile = TILE // IMG_MAX

    @pl.when(step == 0)
    def _():
        gained[...] = hidden_ref[...] * gain_ref[...]
        squares = square_ref[...] + lane_squares(hidden_ref[...])
        mean_square = jnp.sum(squares, axis=-1, keepdims=True) * (1.0 / (2 * depth))
        factor[...] = jnp.broadcast_to(lax.rsqrt(mean_square + rms_epsilon), factor.shape)

    def product():
        heads[lax.rem(step, 2)] = part_ref[...] + jnp.dot(
            gained[...], w_ref[...], preferred_element_type=jnp.float32
        )

    def rotated(values):
        values = values.reshape(per_tile, IMG_MAX, HEAD_SIZE)
        turned = pltpu.roll(values, HEAD_SIZE // 2, 2)
        mixed = values * cos_ref[...][None] + turned * sine_ref[...][None]
        return mixed.reshape(TILE, HEAD_SIZE).astype(jnp.bfloat16)

    def attention(group):
        slot = group % 2
        q_at = lax.broadcasted_iota(jnp.int32, (QUERY_PER_KEY * TILE, TILE), 0)
        k_at = lax.broadcasted_iota(jnp.int32, (QUERY_PER_KEY * TILE, TILE), 1)
        q_at = jnp.bitwise_and(q_at, TILE - 1)
        allowed = (q_at >= k_at) & ((q_at // IMG_MAX) == (k_at // IMG_MAX))
        for tile in range(rows // TILE):
            at = slice(tile * TILE, (tile + 1) * TILE)
            scale = factor[at, :]

            def head(n):
                return heads[slot, at, n * HEAD_SIZE : (n + 1) * HEAD_SIZE] * scale

            queries = jnp.concatenate([rotated(head(n)) for n in range(QUERY_PER_KEY)], axis=0)
            key_rows = rotated(head(QUERY_PER_KEY))
            value_rows = head(QUERY_PER_KEY + 1).astype(jnp.bfloat16)
            scores = lax.dot_general(
                queries, key_rows, (((1,), (1,)), ((), ())), preferred_element_type=jnp.float32
            ) * np.float32(HEAD_SIZE**-0.5)
            scores = jnp.where(allowed, scores, -1e30)
            weights = jnp.exp(scores - jnp.max(scores, axis=-1, keepdims=True))
            inverse = 1.0 / jnp.sum(weights, axis=-1, keepdims=True)
            probabilities = (weights * inverse).astype(jnp.bfloat16)
            attended = jnp.dot(
                probabilities, value_rows, preferred_element_type=jnp.float32
            ).astype(jnp.bfloat16)
            for j in range(per_tile):
                k = tile * per_tile + j
                target = lax.rem(place_ref[0] - shift_ref[k] + senders, senders)
                for n in range(QUERY_PER_KEY):
                    column = (group * QUERY_PER_KEY + n) * HEAD_SIZE
                    out_ref[target, :, column : column + HEAD_SIZE] = attended[
                        n * TILE + j * IMG_MAX : n * TILE + (j + 1) * IMG_MAX, :
                    ]

    groups = pl.num_programs(0) - 1
    del groups

    @pl.when(step == 0)
    def _():
        product()

    @pl.when(step == 1)
    def _():
        product()
        attention(0)

    @pl.when(step == 2)
    def _():
        attention(1)


def attend(place, shift, hidden, rms_gain, w_qkv, part, square, senders):
    rows, depth = hidden.shape
    block = (QUERY_PER_KEY + 2) * HEAD_SIZE
    groups = w_qkv.shape[1] // block
    out_columns = groups * QUERY_PER_KEY * HEAD_SIZE
    cos, sine = rotary_tables()
    whole = lambda j, *_: (0, 0)
    return pl.pallas_call(
        attend_body,
        grid_spec=pltpu.PrefetchScalarGridSpec(
            num_scalar_prefetch=2,
            grid=(groups + 1,),
            in_specs=[
                pl.BlockSpec((rows, depth), whole),
                pl.BlockSpec((1, depth), lambda j, place, shift: (0, 1 - place[1])),
                pl.BlockSpec(
                    (depth, block),
                    lambda j, place, shift: (1 - place[1], jnp.minimum(j, groups - 1)),
                ),
                pl.BlockSpec((rows, block), lambda j, *_: (0, jnp.minimum(j, groups - 1))),
                pl.BlockSpec((rows, 128), whole),
                pl.BlockSpec((IMG_MAX, HEAD_SIZE), whole),
                pl.BlockSpec((IMG_MAX, HEAD_SIZE), whole),
            ],
            out_specs=pl.BlockSpec((senders, IMG_MAX, out_columns), lambda j, *_: (0, 0, 0)),
            scratch_shapes=[
                pltpu.VMEM((rows, depth), jnp.bfloat16),
                pltpu.VMEM((rows, HEAD_SIZE), jnp.float32),
                pltpu.VMEM((2, rows, block), jnp.float32),
            ],
        ),
        out_shape=jax.ShapeDtypeStruct((senders, IMG_MAX, out_columns), jnp.bfloat16),
        compiler_params=pltpu.CompilerParams(vmem_limit_bytes=VMEM_BYTES),
        cost_estimate=pl.CostEstimate(
            flops=2 * rows * depth * groups * block,
            bytes_accessed=2 * depth * groups * block,
            transcendentals=0,
        ),
        name="attend",
    )(place, shift, hidden, rms_gain, w_qkv, part, square, jnp.asarray(cos), jnp.asarray(sine))


def place_body(place_ref, counts_ref, shift_ref, box_ref, out_ref):
    tile = pl.program_id(0)
    senders = box_ref.shape[0]
    images = shift_ref.shape[0]
    per_tile = TILE // IMG_MAX
    lane = lax.broadcasted_iota(jnp.int32, (TILE, TILE), 1)
    row = lax.broadcasted_iota(jnp.int32, (TILE, TILE), 0)
    inside = jnp.bitwise_and(lane, IMG_MAX - 1)
    image = lane // IMG_MAX
    pick = jnp.zeros((TILE, TILE), jnp.bool_)
    offset = jnp.int32(0)
    blocks = []
    for j in range(per_tile):
        k = tile * per_tile + j
        count = counts_ref[place_ref[0] * images + k]
        hit = (image == j) & (row == inside + offset) & (inside < count)
        pick = pick | hit
        offset = offset + count
        source = lax.rem(place_ref[0] + shift_ref[k], senders)
        blocks.append(box_ref[source])
    out_ref[...] = jnp.dot(
        jnp.where(pick, 1.0, 0.0).astype(jnp.bfloat16),
        jnp.concatenate(blocks, axis=0),
        preferred_element_type=jnp.float32,
    ).astype(jnp.bfloat16)


def place_rows(place, counts, shift, box):
    senders, depth, columns = box.shape
    tiles = shift.shape[0] * depth // TILE
    return pl.pallas_call(
        place_body,
        grid_spec=pltpu.PrefetchScalarGridSpec(
            num_scalar_prefetch=3,
            grid=(tiles,),
            in_specs=[pl.BlockSpec((senders, depth, columns), lambda i, *_: (0, 0, 0))],
            out_specs=pl.BlockSpec((TILE, columns), lambda i, *_: (i, 0)),
        ),
        out_shape=jax.ShapeDtypeStruct((tiles * TILE, columns), jnp.bfloat16),
        compiler_params=pltpu.CompilerParams(vmem_limit_bytes=VMEM_BYTES),
        name="place_rows",
    )(place, counts, shift, box)


def local(
    patches, ln_gain, ln_bias, w_proj, proj_bias, rms_gain, w_qkv, image_counts, source_shift
):
    senders = lax.axis_size("dp")
    place = jnp.stack([lax.axis_index("dp"), lax.axis_index("mp")]).astype(jnp.int32)
    counts = image_counts.reshape(-1)
    other = lax.ppermute(patches, "mp", SWAP)
    gain = ln_gain.reshape(1, -1)
    bias = ln_bias.reshape(1, -1)
    own = layer_norm(patches, gain, bias)
    hidden = project(
        place, counts, source_shift, own, other, gain, bias, w_proj, proj_bias.reshape(1, -1)
    )
    far_hidden = lax.ppermute(hidden, "mp", SWAP)
    rms_row = rms_gain.reshape(1, -1)
    part, square = first_half(place, hidden, rms_row, w_qkv)
    outbox = attend(place, source_shift, far_hidden, rms_row, w_qkv, part, square, senders)
    in_box = lax.all_to_all(outbox, "dp", split_axis=0, concat_axis=0, tiled=True)
    return place_rows(place, counts, source_shift, in_box)


def solution(mesh):
    in_specs = (
        P(("dp", "mp"), None),
        P(),
        P(),
        P(None, "mp"),
        P("mp"),
        P(),
        P(None, "mp"),
        P(),
        P(),
    )
    out_specs = P("dp", "mp")
    return jax.shard_map(local, mesh=mesh, in_specs=in_specs, out_specs=out_specs, check_vma=False)
```

time: 187 us -> 109 us (0.58)
  local copies, waits for them, and re-layouts: 65.6 us -> 8.62 us
  Pallas kernels: 0 us -> 56.4 us
  matrix products: 35.6 us -> 0 us
  blocking collectives: 8.18 us -> 41.8 us
  waiting for transfers between devices: 32.9 us -> 0.01 us
  other arithmetic: 26.2 us -> 0.65 us
  starting transfers between devices: 16 us -> 0.51 us
    pallas_call x0 -> x5, Pallas kernels: none -> 56.4 us  [the longest x1 22.6 us: project(): pl.pallas_call(project_body, grid_spec=pltpu.PrefetchScalarGridSpec(num_s...]
    all_to_all x1, blocking collectives: 8.18 us -> 41.8 us  [local(): lax.all_to_all(outbox, 'dp', split_axis=0, concat_axis=0, tiled=True)]
    dot_general x4 -> x0, matrix products: 33.4 us -> none  [the longest x1 19.8 us: local(): jnp.dot(normed, w_proj, preferred_element_type=jnp.float32)]
    all_to_all x2 -> x0, waiting for transfers between devices: 32.9 us -> none  [the longest x1 30.8 us: deliver(): lax.all_to_all(outbox, 'dp', split_axis=0, concat_axis=0, tiled=True)]
    unnamed x40 -> x7, local copies, waits for them, and re-layouts: 19.6 us -> 3.41 us
    all_to_all x2 -> x0, starting transfers between devices: 16 us -> none  [the longest x1 11.9 us: deliver(): lax.all_to_all(outbox, 'dp', split_axis=0, concat_axis=0, tiled=True)]
    gather x5 -> x0, local copies, waits for them, and re-layouts: 14.2 us -> none  [the longest x1 4.22 us: deliver(): arrived = jnp.take(in_box, anchors * pair_slots + slot_rank, axis=0)]
    concatenate x4 -> x0, local copies, waits for them, and re-layouts: 7.4 us -> none  [rotary(): jnp.concatenate([-values[..., half_width:], values[..., :half_width]], ax...]
  transfers between devices with their start and end apart: 2 -> 2, of which waited for: 2 -> 0; matrix products, arithmetic and copies ran while one was open for 14% -> 6% of each run, Pallas kernels for 0% -> 15%
where the time goes in v1:
time: 109 us; the launch traced here: 108 us
  Pallas kernels  56.4 us (52%)
  blocking collectives  41.8 us (38%)
  local copies, waits for them, and re-layouts  8.62 us (8%)
    all_to_all x1, blocking collectives, local(): lax.all_to_all(outbox, 'dp', split_axis=0, concat_axis=0, tiled=True)  41.8 us
    pallas_call x1, Pallas kernels, project(): pl.pallas_call(project_body, grid_spec=pltpu.PrefetchScalarGridSpec(num_s...  22.6 us
    pallas_call x1, Pallas kernels, attend(): pl.pallas_call(attend_body, grid_spec=pltpu.PrefetchScalarGridSpec(num_sc...  12.3 us
    pallas_call x1, Pallas kernels, first_half(): pl.pallas_call(first_half_body, grid_spec=pltpu.PrefetchScalarGridSpec(nu...  9.92 us
    pallas_call x1, Pallas kernels, layer_norm(): pl.pallas_call(norm_body, grid=(count // step,), in_specs=[pl.BlockSpec((...  6.54 us
    pallas_call x1, Pallas kernels, place_rows(): pl.pallas_call(place_body, grid_spec=pltpu.PrefetchScalarGridSpec(num_sca...  5.01 us
    unnamed x7, local copies, waits for them, and re-layouts  3.41 us
  transfers between devices with their start and end apart: 2, of which 0 were waited for; matrix products, arithmetic and copies ran while one was open for 6% of the time, Pallas kernels for 15%

profile of v1, /device:TPU:0, one launch (start us, length us, event | category | flops | bytes accessed | tf_op | source)
XLA Modules:
  0.0 108.0 jit_solution(16448874772806654214)
XLA Ops:
  0.0 0.0 collective-permute-start
  0.0 1.3 %reshape.18.add_ref = bf16[1,2048]{1,0:T(2,128)(2,1)} reshape(bf16[2048]{0:T(1024)(128)(2,1)} %param.15) | data formatting | bytes 8192 | tf_op jit(solution)/shard_map/reshape | solution.py:392
  1.3 1.3 %reshape.16.gain_ref = bf16[1,3200]{1,0:T(2,128)(2,1)} reshape(bf16[3200]{0:T(1024)(128)(2,1)} %param.12) | data formatting | bytes 12800 | tf_op jit(solution)/shard_map/reshape | solution.py:388
  2.6 1.3 %reshape.17.bias_ref = bf16[1,3200]{1,0:T(2,128)(2,1)} reshape(bf16[3200]{0:T(1024)(128)(2,1)} %param.13) | data formatting | bytes 12800 | tf_op jit(solution)/shard_map/reshape | solution.py:389
  3.9 0.8 copy.12
  4.7 0.7 reshape.15.counts_ref
  5.4 6.5 %layer_norm.1.own_ref = bf16[256,3200]{1,0:T(8,128)(2,1)} custom-call(bf16[256,3200]{1,0:T(8,128)(2,1)} %rows_ref.1, bf16[1,3200]{1,0:T(2,128)(2,1)} %reshape.16.gain_ref, bf16[1,3200]{1,0:T(2,128)(2,1)} %reshape.17.bias_ref), custom_call_target="tpu_custom_call" | custom-call | flops 8192000 | bytes 3276800 | tf_op jit(solution)/shard_map/layer_norm/pallas_call | solution.py:50
  12.0 0.7 pad_add_fusion.place_ref
  12.6 0.0 copy-start.1
  12.6 0.0 collective-permute-done.other_ref
  12.6 0.0 copy-start.2
  12.6 1.2 %copy-done.2 = bf16[256,3200]{1,0:T(8,128)(2,1)} copy-done((bf16[256,3200]{1,0:T(8,128)(2,1)}, bf16[256,3200]{1,0:T(8,128)(2,1)S(1)}, u32[]{:S(2)}) %copy-start.2) | copy-done | bytes 1638424
  13.8 22.6 %project.1.hidden_ref = bf16[512,2048]{1,0:T(8,128)(2,1)} custom-call(s32[2]{0:T(128)} %pad_add_fusion.place_ref, s32[2048]{0:T(1024)} %reshape.15.counts_ref, s32[32]{0:T(128)} %shift_ref.5, bf16[256,3200]{1,0:T(8,128)(2,1)} %layer_norm.1.own_ref, bf16[256,3200]{1,0:T(8,128)(2,1)} %copy-done.2, bf16[1,3200]{1,0:T(2,128)(2,1)} %reshape.16.gain_ref, ...), custom_call_target="tpu_custom_call" | custom-call | flops 6710886400 | bytes 13107200 | tf_op jit(solution)/shard_map/project/pallas_call | solution.py:133
  36.4 0.5 collective-permute-start.1
  36.9 0.0 copy-done.1
  36.9 0.6 reshape.19.gain_ref
  37.5 9.9 %first_half.1 = (f32[512,1536]{1,0:T(8,128)}, f32[512,128]{1,0:T(8,128)}) custom-call(s32[2]{0:T(128)} %pad_add_fusion.place_ref, bf16[512,2048]{1,0:T(8,128)(2,1)} %project.1.hidden_ref, bf16[1,4096]{1,0:T(2,128)(2,1)} %reshape.19.gain_ref, bf16[4096,1536]{1,0:T(8,128)(2,1)} %w_ref.5), custom_call_target="tpu_custom_call" | custom-call | flops 3221225472 | bytes 9437184 | tf_op jit(solution)/shard_map/first_half/pallas_call | solution.py:185
  47.5 0.0 collective-permute-done.1.hidden_ref
  47.5 0.0 copy-start
  47.5 1.4 %copy-done = bf16[512,2048]{1,0:T(8,128)(2,1)} copy-done((bf16[512,2048]{1,0:T(8,128)(2,1)}, bf16[512,2048]{1,0:T(8,128)(2,1)S(1)}, u32[]{:S(2)}) %copy-start) | copy-done | bytes 2097176
  48.8 12.3 %attend.1 = bf16[64,16,1024]{2,1,0:T(8,128)(2,1)} custom-call(s32[2]{0:T(128)} %pad_add_fusion.place_ref, s32[32]{0:T(128)} %shift_ref.5, bf16[512,2048]{1,0:T(8,128)(2,1)} %copy-done, bf16[1,4096]{1,0:T(2,128)(2,1)} %reshape.19.gain_ref, bf16[4096,1536]{1,0:T(8,128)(2,1)} %w_ref.5, f32[512,1536]{1,0:T(8,128)} %get-tuple-element.7.part_ref, ...), custom_call_target="tpu_custom_call" | custom-call | flops 3221225472 | bytes 6291456 | tf_op jit(solution)/shard_map/attend/pallas_call | solution.py:302
  61.2 41.8 %all_to_all.5.box_ref = bf16[64,16,1024]{2,1,0:T(8,128)(2,1)} all-to-all(bf16[64,16,1024]{2,1,0:T(8,128)(2,1)} %attend.1), channel_id=1, replica_groups=mesh['dp'=64,'mp'=2] {'dp'}, dimensions={0} | all-to-all | bytes 4194304 | tf_op jit(solution)/shard_map/all_to_all | solution.py:398
  103.0 5.0 %place_rows.1 = bf16[512,1024]{1,0:T(8,128)(2,1)} custom-call(s32[2]{0:T(128)} %pad_add_fusion.place_ref, s32[2048]{0:T(1024)} %reshape.15.counts_ref, s32[32]{0:T(128)} %shift_ref.5, bf16[64,16,1024]{2,1,0:T(8,128)(2,1)} %all_to_all.5.box_ref), custom_call_target="tpu_custom_call" | custom-call | tf_op jit(solution)/shard_map/place_rows/pallas_call | solution.py:367
Async XLA Ops:
  0.0 12.6 %collective-permute-start = (bf16[256,3200]{1,0:T(8,128)(2,1)}, bf16[256,3200]{1,0:T(8,128)(2,1)S(1)}, u32[]{:S(2)}, u32[]{:S(2)}) collective-permute-start(bf16[256,3200]{1,0:T(8,128)(2,1)} %rows_ref.1), channel_id=1, source_target_pairs={{0,1},{1,0},{2,3},{3,2},{4,5},{5,4},{6,7},{7,6},{8,9},{9,8},{10,11... | collective-permute-start | bytes 4915208 | tf_op jit(solution)/shard_map/ppermute | solution.py:387
  12.6 24.3 %copy-start.1 = (bf16[4096]{0:T(1024)(128)(2,1)S(1)}, bf16[4096]{0:T(1024)(128)(2,1)}, u32[]{:S(2)}) copy-start(bf16[4096]{0:T(1024)(128)(2,1)} %param.16) | copy-start | bytes 24580
  12.6 1.2 %copy-start.2 = (bf16[256,3200]{1,0:T(8,128)(2,1)}, bf16[256,3200]{1,0:T(8,128)(2,1)S(1)}, u32[]{:S(2)}) copy-start(bf16[256,3200]{1,0:T(8,128)(2,1)S(1)} %collective-permute-done.other_ref) | copy-start | bytes 4915204
  36.4 11.0 %collective-permute-start.1 = (bf16[512,2048]{1,0:T(8,128)(2,1)}, bf16[512,2048]{1,0:T(8,128)(2,1)S(1)}, u32[]{:S(2)}, u32[]{:S(2)}) collective-permute-start(bf16[512,2048]{1,0:T(8,128)(2,1)} %project.1.hidden_ref), channel_id=1, source_target_pairs={{0,1},{1,0},{2,3},{3,2},{4,5},{5,4},{6,7},{7,6},{8,9},{9,8},{10,11... | collective-permute-start | bytes 6291464 | tf_op jit(solution)/shard_map/ppermute | solution.py:394
  47.5 1.4 %copy-start = (bf16[512,2048]{1,0:T(8,128)(2,1)}, bf16[512,2048]{1,0:T(8,128)(2,1)S(1)}, u32[]{:S(2)}) copy-start(bf16[512,2048]{1,0:T(8,128)(2,1)S(1)} %collective-permute-done.1.hidden_ref) | copy-start | bytes 6291460

commit v2 on v1

v2 whole, which is shorter than its diff:
```python
import functools

import jax
import jax.numpy as jnp
import numpy as np
from jax import lax
from jax.experimental import pallas as pl
from jax.experimental.pallas import tpu as pltpu
from jax.sharding import PartitionSpec as P

HEAD_SIZE = 128
TILE = 128
QUERY_PER_KEY = 4
IMG_MAX = 16

norm_epsilon = 1e-05
rms_epsilon = 1e-05
rotary_base = 500000.0

SWAP = [(0, 1), (1, 0)]


def rotary_tables():
    half = HEAD_SIZE // 2
    frequency = rotary_base ** (-(np.arange(half, dtype=np.float64) * (2.0 / HEAD_SIZE)))
    angles = np.arange(IMG_MAX, dtype=np.float64)[:, None] * frequency[None, :]
    cos = np.concatenate([np.cos(angles), np.cos(angles)], axis=-1)
    sine = np.concatenate([-np.sin(angles), np.sin(angles)], axis=-1)
    return cos.astype(np.float32), sine.astype(np.float32)


def normalised(rows, gain, bias):
    values = rows.astype(jnp.float32)
    width = values.shape[-1]
    row_mean = jnp.sum(values, axis=-1, keepdims=True) * (1.0 / width)
    centred = values - row_mean
    row_var = jnp.sum(centred * centred, axis=-1, keepdims=True) * (1.0 / width)
    scaled = centred * lax.rsqrt(row_var + norm_epsilon) * gain.astype(jnp.float32)
    return (scaled + bias.astype(jnp.float32)).astype(jnp.bfloat16)


WHOLE = pl.BlockSpec(memory_space=pltpu.VMEM)
SCALARS = pl.BlockSpec(memory_space=pltpu.SMEM)
NORM_ROWS = 32
COLUMNS = 256


def limit(mib):
    return pltpu.CompilerParams(vmem_limit_bytes=mib * 1024 * 1024)


def fill_normed(src_ref, gain_ref, bias_ref, dst_ref, base):
    width = src_ref.shape[1]
    gain = gain_ref[...].reshape(1, width)
    bias = bias_ref[...].reshape(1, width)

    def fill(i, carry):
        src = pl.multiple_of(i * NORM_ROWS, NORM_ROWS)
        dst = pl.multiple_of(base + i * NORM_ROWS, NORM_ROWS)
        dst_ref[pl.ds(dst, NORM_ROWS), :] = normalised(
            src_ref[pl.ds(src, NORM_ROWS), :], gain, bias
        )
        return carry

    lax.fori_loop(0, src_ref.shape[0] // NORM_ROWS, fill, 0)


def norm_body(rows_ref, gain_ref, bias_ref, out_ref):
    fill_normed(rows_ref, gain_ref, bias_ref, out_ref, 0)


def layer_norm(rows, gain, bias):
    count, width = rows.shape
    return pl.pallas_call(
        norm_body,
        in_specs=[WHOLE] * 3,
        out_specs=WHOLE,
        out_shape=jax.ShapeDtypeStruct((count, width), jnp.bfloat16),
        compiler_params=limit(8),
        cost_estimate=pl.CostEstimate(
            flops=6_000_000_000, bytes_accessed=4 * count * width, transcendentals=0
        ),
        name="layer_norm",
    )(rows, gain, bias)


def project_body(
    counts_ref, shift_ref, own_ref, other_ref, gain_ref, bias_ref, w_ref, add_ref,
    out_ref, normed, align, acc_even, acc_odd,
):
    half = own_ref.shape[0]
    rows = 2 * half
    images = shift_ref.shape[0]
    tile_images = counts_ref.shape[0]
    tiles = images // tile_images
    senders = counts_ref.shape[1] // tiles
    blocks = w_ref.shape[1] // COLUMNS
    core = lax.axis_index("mp")
    me = lax.axis_index("dp")

    normed[pl.ds(pl.multiple_of(core * half, half), half), :] = own_ref[...]
    fill_normed(other_ref, gain_ref, bias_ref, normed, (1 - core) * half)
    column = lax.broadcasted_iota(jnp.int32, (IMG_MAX, rows), 1)
    inside = lax.broadcasted_iota(jnp.int32, (IMG_MAX, rows), 0)
    distance = column - inside
    start = jnp.int32(0)
    for k in range(images):
        align[k * IMG_MAX : (k + 1) * IMG_MAX, :] = jnp.where(distance == start, 1.0, 0.0).astype(
            jnp.bfloat16
        )
        target = lax.rem(me - shift_ref[k] + senders, senders)
        start = start + counts_ref[k % tile_images, target * tiles + k // tile_images]

    def product(block, acc):
        at = pl.multiple_of(block * COLUMNS, COLUMNS)
        acc[...] = jnp.dot(
            normed[...], w_ref[:, pl.ds(at, COLUMNS)], preferred_element_type=jnp.float32
        )

    def post(block, acc):
        at = pl.multiple_of(block * COLUMNS, COLUMNS)
        pre = acc[...] + add_ref[:, pl.ds(at, COLUMNS)].astype(jnp.float32)
        value = pre * (1.0 + lax.erf(pre * np.float32(0.5**0.5))) * 0.5
        out_ref[:, pl.ds(at, COLUMNS)] = jnp.dot(
            align[...], value.astype(jnp.bfloat16), preferred_element_type=jnp.float32
        ).astype(jnp.bfloat16)

    acc_odd[...] = jnp.zeros_like(acc_odd)

    def pair(p, carry):
        product(2 * p, acc_even)
        post(jnp.maximum(2 * p - 1, 0), acc_odd)
        product(2 * p + 1, acc_odd)
        post(2 * p, acc_even)
        return carry

    lax.fori_loop(0, blocks // 2, pair, 0)
    post(blocks - 1, acc_odd)


def project(counts, shift, own, other, gain, bias, w_proj, proj_bias):
    half, width = own.shape
    rows = 2 * half
    columns = w_proj.shape[1]
    return pl.pallas_call(
        project_body,
        in_specs=[SCALARS] * 2 + [WHOLE] * 6,
        out_specs=WHOLE,
        scratch_shapes=[
            pltpu.VMEM((rows, width), jnp.bfloat16),
            pltpu.VMEM((rows, rows), jnp.bfloat16),
            pltpu.VMEM((rows, COLUMNS), jnp.float32),
            pltpu.VMEM((rows, COLUMNS), jnp.float32),
        ],
        out_shape=jax.ShapeDtypeStruct((rows, columns), jnp.bfloat16),
        compiler_params=limit(12),
        cost_estimate=pl.CostEstimate(
            flops=2 * rows * width * columns,
            bytes_accessed=2 * width * columns,
            transcendentals=rows * columns,
        ),
        name="project",
    )(counts, shift, own, other, gain, bias, w_proj, proj_bias)


def lane_squares(values):
    total = None
    for c in range(values.shape[1] // 128):
        piece = values[:, c * 128 : (c + 1) * 128].astype(jnp.float32)
        total = piece * piece if total is None else total + piece * piece
    return total


def first_half_body(hidden_ref, gain_ref, w_ref, part_ref, square_ref, gained):
    depth = hidden_ref.shape[1]
    mine = pl.multiple_of(lax.axis_index("mp") * depth, depth)
    gained[...] = hidden_ref[...] * gain_ref[:, pl.ds(mine, depth)]
    square_ref[...] = lane_squares(hidden_ref[...])

    def block(j, carry):
        at = pl.multiple_of(j * COLUMNS, COLUMNS)
        part_ref[:, pl.ds(at, COLUMNS)] = jnp.dot(
            gained[...], w_ref[pl.ds(mine, depth), pl.ds(at, COLUMNS)],
            preferred_element_type=jnp.float32,
        )
        return carry

    lax.fori_loop(0, w_ref.shape[1] // COLUMNS, block, 0)


def first_half(hidden, rms_gain, w_qkv):
    rows, depth = hidden.shape
    columns = w_qkv.shape[1]
    return pl.pallas_call(
        first_half_body,
        in_specs=[WHOLE] * 3,
        out_specs=[WHOLE] * 2,
        scratch_shapes=[pltpu.VMEM((rows, depth), jnp.bfloat16)],
        out_shape=[
            jax.ShapeDtypeStruct((rows, columns), jnp.float32),
            jax.ShapeDtypeStruct((rows, 128), jnp.float32),
        ],
        compiler_params=limit(8),
        cost_estimate=pl.CostEstimate(
            flops=2 * rows * depth * columns,
            bytes_accessed=2 * depth * columns + 4 * rows * columns,
            transcendentals=0,
        ),
        name="first_half",
    )(hidden, rms_gain, w_qkv)


def attend_body(
    shift_ref, hidden_ref, gain_ref, w_ref, part_ref, square_ref, cos_ref, sine_ref,
    out_ref, gained, factor, *heads,
):
    rows, depth = hidden_ref.shape
    senders = out_ref.shape[0]
    per_tile = TILE // IMG_MAX
    width = heads[0].shape[1]
    me = lax.axis_index("dp")
    far = pl.multiple_of((1 - lax.axis_index("mp")) * depth, depth)

    gained[...] = hidden_ref[...] * gain_ref[:, pl.ds(far, depth)]
    squares = square_ref[...] + lane_squares(hidden_ref[...])
    mean_square = jnp.sum(squares, axis=-1, keepdims=True) * (1.0 / (2 * depth))
    factor[...] = jnp.broadcast_to(lax.rsqrt(mean_square + rms_epsilon), factor.shape)

    def product(group):
        at = slice(group * width, (group + 1) * width)
        heads[group][...] = part_ref[:, at] + jnp.dot(
            gained[...], w_ref[pl.ds(far, depth), at], preferred_element_type=jnp.float32
        )

    def rotated(values):
        values = values.reshape(per_tile, IMG_MAX, HEAD_SIZE)
        turned = pltpu.roll(values, HEAD_SIZE // 2, 2)
        mixed = values * cos_ref[...][None] + turned * sine_ref[...][None]
        return mixed.reshape(TILE, HEAD_SIZE).astype(jnp.bfloat16)

    q_at = lax.broadcasted_iota(jnp.int32, (QUERY_PER_KEY * TILE, TILE), 0)
    k_at = lax.broadcasted_iota(jnp.int32, (QUERY_PER_KEY * TILE, TILE), 1)
    q_at = jnp.bitwise_and(q_at, TILE - 1)
    allowed = (q_at >= k_at) & ((q_at // IMG_MAX) == (k_at // IMG_MAX))

    def attention(group):
        for tile in range(rows // TILE):
            at = slice(tile * TILE, (tile + 1) * TILE)
            scale = factor[at, :]

            def head(n):
                return heads[group][at, n * HEAD_SIZE : (n + 1) * HEAD_SIZE] * scale

            queries = jnp.concatenate([rotated(head(n)) for n in range(QUERY_PER_KEY)], axis=0)
            key_rows = rotated(head(QUERY_PER_KEY))
            value_rows = head(QUERY_PER_KEY + 1).astype(jnp.bfloat16)
            scores = lax.dot_general(
                queries, key_rows, (((1,), (1,)), ((), ())), preferred_element_type=jnp.float32
            ) * np.float32(HEAD_SIZE**-0.5)
            scores = jnp.where(allowed, scores, -1e30)
            weights = jnp.exp(scores - jnp.max(scores, axis=-1, keepdims=True))
            inverse = 1.0 / jnp.sum(weights, axis=-1, keepdims=True)
            probabilities = (weights * inverse).astype(jnp.bfloat16)
            attended = jnp.dot(
                probabilities, value_rows, preferred_element_type=jnp.float32
            ).astype(jnp.bfloat16)
            for j in range(per_tile):
                target = lax.rem(me - shift_ref[tile * per_tile + j] + senders, senders)
                for n in range(QUERY_PER_KEY):
                    column = (group * QUERY_PER_KEY + n) * HEAD_SIZE
                    out_ref[target, :, column : column + HEAD_SIZE] = attended[
                        n * TILE + j * IMG_MAX : n * TILE + (j + 1) * IMG_MAX, :
                    ]

    product(0)
    for group in range(1, len(heads)):
        product(group)
        attention(group - 1)
    attention(len(heads) - 1)


def attend(shift, hidden, rms_gain, w_qkv, part, square, senders):
    rows, depth = hidden.shape
    block = (QUERY_PER_KEY + 2) * HEAD_SIZE
    groups = w_qkv.shape[1] // block
    out_columns = groups * QUERY_PER_KEY * HEAD_SIZE
    cos, sine = rotary_tables()
    return pl.pallas_call(
        attend_body,
        in_specs=[SCALARS] + [WHOLE] * 7,
        out_specs=WHOLE,
        scratch_shapes=[
            pltpu.VMEM((rows, depth), jnp.bfloat16),
            pltpu.VMEM((rows, HEAD_SIZE), jnp.float32),
        ]
        + [pltpu.VMEM((rows, block), jnp.float32)] * groups,
        out_shape=jax.ShapeDtypeStruct((senders, IMG_MAX, out_columns), jnp.bfloat16),
        compiler_params=limit(10),
        cost_estimate=pl.CostEstimate(
            flops=2 * rows * depth * groups * block,
            bytes_accessed=2 * depth * groups * block,
            transcendentals=0,
        ),
        name="attend",
    )(shift, hidden, rms_gain, w_qkv, part, square, jnp.asarray(cos), jnp.asarray(sine))


def place_body(counts_ref, shift_ref, box_ref, out_ref):
    senders = box_ref.shape[0]
    per_tile = counts_ref.shape[0]
    tiles = shift_ref.shape[0] // per_tile
    me = lax.axis_index("dp")
    lane = lax.broadcasted_iota(jnp.int32, (TILE, TILE), 1)
    row = lax.broadcasted_iota(jnp.int32, (TILE, TILE), 0)
    inside = jnp.bitwise_and(lane, IMG_MAX - 1)
    image = lane // IMG_MAX
    for tile in range(tiles):
        goal = jnp.full((TILE, TILE), -1, jnp.int32)
        offset = jnp.int32(0)
        blocks = []
        for j in range(per_tile):
            count = counts_ref[j, me * tiles + tile]
            goal = jnp.where((image == j) & (inside < count), inside + offset, goal)
            offset = offset + count
            source = lax.rem(me + shift_ref[tile * per_tile + j], senders)
            blocks.append(box_ref[source])
        out_ref[tile * TILE : (tile + 1) * TILE, :] = jnp.dot(
            jnp.where(row == goal, 1.0, 0.0).astype(jnp.bfloat16),
            jnp.concatenate(blocks, axis=0),
            preferred_element_type=jnp.float32,
        ).astype(jnp.bfloat16)


def place_rows(counts, shift, box):
    senders, depth, columns = box.shape
    rows = shift.shape[0] * depth
    return pl.pallas_call(
        place_body,
        in_specs=[SCALARS] * 2 + [WHOLE],
        out_specs=WHOLE,
        out_shape=jax.ShapeDtypeStruct((rows, columns), jnp.bfloat16),
        compiler_params=limit(8),
        name="place_rows",
    )(counts, shift, box)


def local(
    patches, ln_gain, ln_bias, w_proj, proj_bias, rms_gain, w_qkv, image_counts, source_shift
):
    senders = lax.axis_size("dp")
    counts = image_counts.T
    other = lax.ppermute(patches, "mp", SWAP)
    own = layer_norm(patches, ln_gain, ln_bias)
    hidden = project(
        counts, source_shift, own, other, ln_gain, ln_bias, w_proj, proj_bias.reshape(1, -1)
    )
    far_hidden = lax.ppermute(hidden, "mp", SWAP)
    rms_row = rms_gain.reshape(1, -1)
    part, square = first_half(hidden, rms_row, w_qkv)
    outbox = attend(source_shift, far_hidden, rms_row, w_qkv, part, square, senders)
    in_box = lax.all_to_all(outbox, "dp", split_axis=0, concat_axis=0, tiled=True)
    return place_rows(counts, source_shift, in_box)


def solution(mesh):
    in_specs = (
        P(("dp", "mp"), None),
        P(),
        P(),
        P(None, "mp"),
        P("mp"),
        P(),
        P(None, "mp"),
        P(),
        P(),
    )
    out_specs = P("dp", "mp")
    return jax.shard_map(local, mesh=mesh, in_specs=in_specs, out_specs=out_specs, check_vma=False)
```

time: 109 us -> 76.7 us (0.70)
  Pallas kernels: 56.4 us -> 28.3 us
  local copies, waits for them, and re-layouts: 8.62 us -> 5.83 us
    pallas_call x5, Pallas kernels: 56.4 us -> 28.3 us  [the longest x1 12.8 us: project(): pl.pallas_call(project_body, in_specs=[SCALARS] * 2 + [WHOLE] * 6, out_sp...]
    reshape x3 -> x0, local copies, waits for them, and re-layouts: 3.31 us -> none  [the longest x1 1.3 us: local(): gain = ln_gain.reshape(1, -1)]
    unnamed x7 -> x28, local copies, waits for them, and re-layouts: 3.41 us -> 5.13 us
  transfers between devices with their start and end apart: 2 -> 2, of which waited for: 0 -> 0; matrix products, arithmetic and copies ran while one was open for 6% -> 1% of each run, Pallas kernels for 15% -> 10%
where the time goes in v2:
time: 76.7 us; the launch traced here: 76.4 us
  blocking collectives  41.6 us (54%)
  Pallas kernels  28.3 us (37%)
  local copies, waits for them, and re-layouts  5.83 us (8%)
    all_to_all x1, blocking collectives, local(): lax.all_to_all(outbox, 'dp', split_axis=0, concat_axis=0, tiled=True)  41.6 us
    pallas_call x1, Pallas kernels, project(): pl.pallas_call(project_body, in_specs=[SCALARS] * 2 + [WHOLE] * 6, out_sp...  12.8 us
    pallas_call x1, Pallas kernels, attend(): pl.pallas_call(attend_body, in_specs=[SCALARS] + [WHOLE] * 7, out_specs=W...  6.07 us
    unnamed x28, local copies, waits for them, and re-layouts  5.13 us
    pallas_call x1, Pallas kernels, first_half(): pl.pallas_call(first_half_body, in_specs=[WHOLE] * 3, out_specs=[WHOLE] *...  4.87 us
    pallas_call x1, Pallas kernels, layer_norm(): pl.pallas_call(norm_body, in_specs=[WHOLE] * 3, out_specs=WHOLE, out_shap...  2.43 us
    pallas_call x1, Pallas kernels, place_rows(): pl.pallas_call(place_body, in_specs=[SCALARS] * 2 + [WHOLE], out_specs=WH...  2.09 us
  transfers between devices with their start and end apart: 2, of which 0 were waited for; matrix products, arithmetic and copies ran while one was open for 1% of the time, Pallas kernels for 10%

profile of v2, /device:TPU:0, one launch (start us, length us, event | category | flops | bytes accessed | tf_op | source)
XLA Modules:
  0.0 76.4 jit_solution(7520824574717532003)
XLA Ops:
  0.0 0.0 collective-permute-start
  0.0 0.7 reshape.6.add_ref
  0.7 0.0 copy-start.5
  0.7 1.4 %copy-done.5 = bf16[256,3200]{1,0:T(8,128)(2,1)S(1)} copy-done((bf16[256,3200]{1,0:T(8,128)(2,1)S(1)}, bf16[256,3200]{1,0:T(8,128)(2,1)}, u32[]{:S(2)}) %copy-start.5) | copy-done | bytes 1638424
  2.1 0.0 copy-start.6
  2.1 0.7 copy-done.6
  2.8 0.0 copy-start.8
  2.8 0.7 copy-done.8
  3.5 0.0 copy-start
  3.5 0.0 copy-start.3
  3.5 0.0 copy-start.4
  3.5 0.0 copy-start.7
  3.5 0.0 copy-start.9
  3.5 2.4 %layer_norm.1.own_ref = bf16[256,3200]{1,0:T(8,128)(2,1)S(1)} custom-call(bf16[256,3200]{1,0:T(8,128)(2,1)S(1)} %copy-done.5, bf16[3200]{0:T(1024)(128)(2,1)S(1)} %copy-done.6, bf16[3200]{0:T(1024)(128)(2,1)S(1)} %copy-done.8), custom_call_target="tpu_custom_call" | custom-call | flops 6000000000 | bytes 3276800 | tf_op jit(solution)/shard_map/layer_norm/pallas_call | solution.py:74
  6.0 0.0 collective-permute-done.other_ref
  6.0 0.0 slice-start
  6.0 0.0 copy-done
  6.0 0.0 copy-done.3
  6.0 2.3 %copy-done.4 = bf16[3200,2048]{1,0:T(8,128)(2,1)S(1)} copy-done((bf16[3200,2048]{1,0:T(8,128)(2,1)S(1)}, bf16[3200,2048]{1,0:T(8,128)(2,1)}, u32[]{:S(2)}) %copy-start.4) | copy-done | bytes 13107224
  8.3 0.0 copy-done.7
  8.3 0.0 copy-done.9
  8.3 0.0 copy-start.10
  8.3 0.0 slice-start.1
  8.3 0.0 slice-start.2
  8.3 12.8 %project.1.hidden_ref = bf16[512,2048]{1,0:T(8,128)(2,1)S(1)} custom-call(s32[8,256]{1,0:T(8,128)S(1)} %bitcast.3, s32[32]{0:T(128)S(1)} %copy-done.3, bf16[256,3200]{1,0:T(8,128)(2,1)S(1)} %layer_norm.1.own_ref, bf16[256,3200]{1,0:T(8,128)(2,1)S(1)} %collective-permute-done.other_ref, bf16[3200]{0:T(1024)(128)(2,1)S(1)} %copy-done.7, ...), custom_call_target="tpu_custom_call" | custom-call | flops 6710886400 | bytes 13107200 | tf_op jit(solution)/shard_map/project/pallas_call | solution.py:145
  21.2 0.6 collective-permute-start.1
  21.7 0.0 copy-done.10
  21.8 0.0 slice-done
  21.8 0.0 slice-done.1
  21.8 0.0 slice-done.2
  21.8 0.0 copy-start.1
  21.8 0.0 copy-start.2
  21.8 4.9 %first_half.1 = (f32[512,1536]{1,0:T(8,128)S(1)}, f32[512,128]{1,0:T(8,128)S(1)}) custom-call(bf16[512,2048]{1,0:T(8,128)(2,1)S(1)} %project.1.hidden_ref, bf16[1,4096]{1,0:T(2,128)(2,1)S(1)} %reshape.7.gain_ref, bf16[4096,1536]{1,0:T(8,128)(2,1)S(1)} %bitcast.2), custom_call_target="tpu_custom_call" | custom-call | flops 3221225472 | bytes 9437184 | tf_op jit(solution)/shard_map/first_half/pallas_call | solution.py:194
  26.7 0.0 collective-permute-done.1.hidden_ref
  26.7 0.0 copy-done.1
  26.7 0.0 copy-done.2
  26.7 6.1 %attend.1 = bf16[64,16,1024]{2,1,0:T(8,128)(2,1)S(1)} custom-call(s32[32]{0:T(128)S(1)} %copy-done.3, bf16[512,2048]{1,0:T(8,128)(2,1)S(1)} %collective-permute-done.1.hidden_ref, bf16[1,4096]{1,0:T(2,128)(2,1)S(1)} %reshape.7.gain_ref, bf16[4096,1536]{1,0:T(8,128)(2,1)S(1)} %bitcast.2, f32[512,1536]{1,0:T(8,128)S(1)} %get-tuple-element.7.part_ref, ...), custom_call_target="tpu_custom_call" | custom-call | flops 3221225472 | bytes 6291456 | tf_op jit(solution)/shard_map/attend/pallas_call | solution.py:288
  32.8 41.6 %all_to_all.5.box_ref = bf16[64,16,1024]{2,1,0:T(8,128)(2,1)S(1)} all-to-all(bf16[64,16,1024]{2,1,0:T(8,128)(2,1)S(1)} %attend.1), channel_id=1, replica_groups=mesh['dp'=64,'mp'=2] {'dp'}, dimensions={0} | all-to-all | bytes 4194304 | tf_op jit(solution)/shard_map/all_to_all | solution.py:361
  74.4 2.1 %place_rows.1 = bf16[512,1024]{1,0:T(8,128)(2,1)} custom-call(s32[8,256]{1,0:T(8,128)S(1)} %bitcast.4, s32[32]{0:T(128)S(1)} %copy-done.3, bf16[64,16,1024]{2,1,0:T(8,128)(2,1)S(1)} %all_to_all.5.box_ref), custom_call_target="tpu_custom_call" | custom-call | tf_op jit(solution)/shard_map/place_rows/pallas_call | solution.py:337
  (2 shorter events, 0.0 us)
Async XLA Ops:
  0.0 6.0 %collective-permute-start = (bf16[256,3200]{1,0:T(8,128)(2,1)}, bf16[256,3200]{1,0:T(8,128)(2,1)S(1)}, u32[]{:S(2)}, u32[]{:S(2)}) collective-permute-start(bf16[256,3200]{1,0:T(8,128)(2,1)} %rows_ref.1), channel_id=1, source_target_pairs={{0,1},{1,0},{2,3},{3,2},{4,5},{5,4},{6,7},{7,6},{8,9},{9,8},{10,11... | collective-permute-start | bytes 4915208 | tf_op jit(solution)/shard_map/ppermute | solution.py:352
  0.7 1.4 %copy-start.5 = (bf16[256,3200]{1,0:T(8,128)(2,1)S(1)}, bf16[256,3200]{1,0:T(8,128)(2,1)}, u32[]{:S(2)}) copy-start(bf16[256,3200]{1,0:T(8,128)(2,1)} %rows_ref.1) | copy-start | bytes 4915204
  2.1 0.7 copy-start.6
  2.8 0.7 copy-start.8
  3.5 2.5 %copy-start = (s32[256,8]{0,1:T(8,128)S(1)}, s32[256,8]{0,1:T(8,128)}, u32[]{:S(2)}) copy-start(s32[256,8]{0,1:T(8,128)} %param.18) | copy-start | bytes 24580
  3.5 2.5 %copy-start.3 = (s32[32]{0:T(128)S(1)}, s32[32]{0:T(128)}, u32[]{:S(2)}) copy-start(s32[32]{0:T(128)} %shift_ref.5) | copy-start | bytes 388
  3.5 4.8 %copy-start.4 = (bf16[3200,2048]{1,0:T(8,128)(2,1)S(1)}, bf16[3200,2048]{1,0:T(8,128)(2,1)}, u32[]{:S(2)}) copy-start(bf16[3200,2048]{1,0:T(8,128)(2,1)} %w_ref.3) | copy-start | bytes 39321604
  3.5 4.8 %copy-start.7 = (bf16[3200]{0:T(1024)(128)(2,1)S(1)}, bf16[3200]{0:T(1024)(128)(2,1)}, u32[]{:S(2)}) copy-start(bf16[3200]{0:T(1024)(128)(2,1)} %gain_ref.3) | copy-start | bytes 19204
  3.5 4.8 %copy-start.9 = (bf16[3200]{0:T(1024)(128)(2,1)S(1)}, bf16[3200]{0:T(1024)(128)(2,1)}, u32[]{:S(2)}) copy-start(bf16[3200]{0:T(1024)(128)(2,1)} %bias_ref.3) | copy-start | bytes 19204
  6.0 15.8 %slice-start = ((s8[12582912]{0:T(1024)(128)(4,1)}), s8[4194304]{0:T(1024)(128)(4,1)S(1)}, s32[]{:S(2)}) async-start(s8[12582912]{0:T(1024)(128)(4,1)} %bitcast.1), calls=%async_computation.1 | async-start | bytes 8388608
  8.3 13.5 %copy-start.10 = (bf16[4096]{0:T(1024)(128)(2,1)S(1)}, bf16[4096]{0:T(1024)(128)(2,1)}, u32[]{:S(2)}) copy-start(bf16[4096]{0:T(1024)(128)(2,1)} %param.16) | copy-start | bytes 24580
  8.3 13.5 %slice-start.1 = ((s8[12582912]{0:T(1024)(128)(4,1)}), s8[4194304]{0:T(1024)(128)(4,1)S(1)}, s32[]{:S(2)}) async-start(s8[12582912]{0:T(1024)(128)(4,1)} %bitcast.1), calls=%async_computation.2 | async-start | bytes 8388608
  8.3 13.5 %slice-start.2 = ((s8[12582912]{0:T(1024)(128)(4,1)}), s8[4194304]{0:T(1024)(128)(4,1)S(1)}, s32[]{:S(2)}) async-start(s8[12582912]{0:T(1024)(128)(4,1)} %bitcast.1), calls=%async_computation.3 | async-start | bytes 8388608
  21.2 5.5 %collective-permute-start.1 = (bf16[512,2048]{1,0:T(8,128)(2,1)S(1)}, bf16[512,2048]{1,0:T(8,128)(2,1)S(1)}, u32[]{:S(2)}, u32[]{:S(2)}) collective-permute-start(bf16[512,2048]{1,0:T(8,128)(2,1)S(1)} %project.1.hidden_ref), channel_id=1, source_target_pairs={{0,1},{1,0},{2,3},{3,2},{4,5},{5,4},{6,7},{7,6},{8,9},{9,8},{10,11... | collective-permute-start | bytes 6291464 | tf_op jit(solution)/shard_map/ppermute | solution.py:357
  21.8 4.9 %copy-start.1 = (f32[16,128]{1,0:T(8,128)S(1)}, f32[16,128]{1,0:T(8,128)}, u32[]{:S(2)}) copy-start(f32[16,128]{1,0:T(8,128)} %constant.5.clone.sine_ref) | copy-start | bytes 24580
  21.8 4.9 %copy-start.2 = (f32[16,128]{1,0:T(8,128)S(1)}, f32[16,128]{1,0:T(8,128)}, u32[]{:S(2)}) copy-start(f32[16,128]{1,0:T(8,128)} %constant.4.clone.cos_ref) | copy-start | bytes 24580

commit v3 on v2

v3 whole, which is shorter than its diff:
```python
import functools

import jax
import jax.numpy as jnp
import numpy as np
from jax import lax
from jax.experimental import pallas as pl
from jax.experimental.pallas import tpu as pltpu
from jax.sharding import PartitionSpec as P

HEAD_SIZE = 128
TILE = 128
QUERY_PER_KEY = 4
IMG_MAX = 16

norm_epsilon = 1e-05
rms_epsilon = 1e-05
rotary_base = 500000.0

SWAP = [(0, 1), (1, 0)]


WHOLE = pl.BlockSpec(memory_space=pltpu.VMEM)
SCALARS = pl.BlockSpec(memory_space=pltpu.SMEM)
FAR_MEMORY = pl.BlockSpec(memory_space=pltpu.HBM)
NORM_ROWS = 32
COLUMNS = 256
ROW_BOUNDS = (352, 384)


def limit(mib):
    return pltpu.CompilerParams(vmem_limit_bytes=mib * 1024 * 1024)


def rotary_tables(rows):
    half = HEAD_SIZE // 2
    frequency = rotary_base ** (-(np.arange(half, dtype=np.float64) * (2.0 / HEAD_SIZE)))
    angles = np.arange(rows, dtype=np.float64)[:, None] * frequency[None, :]
    cos = np.concatenate([np.cos(angles), np.cos(angles)], axis=-1)
    sine = np.concatenate([-np.sin(angles), np.sin(angles)], axis=-1)
    return jnp.asarray(cos.astype(np.float32)), jnp.asarray(sine.astype(np.float32))


def image_starts(counts_ref, shift_ref):
    images = shift_ref.shape[0]
    tile_images = counts_ref.shape[0]
    tiles = images // tile_images
    senders = counts_ref.shape[1] // tiles
    me = lax.axis_index("dp")
    starts = []
    start = jnp.int32(0)
    for k in range(images):
        starts.append(start)
        target = lax.rem(me - shift_ref[k] + senders, senders)
        start = start + counts_ref[k % tile_images, target * tiles + k // tile_images]
    return starts, start


def for_row_bound(total, most, run):
    below = jnp.int32(-1)
    for bound in (*ROW_BOUNDS, most):
        pl.when((total > below) & (total <= bound))(functools.partial(run, bound))
        below = jnp.int32(bound)


def normalised(rows, gain, bias):
    values = rows.astype(jnp.float32)
    width = values.shape[-1]
    row_mean = jnp.sum(values, axis=-1, keepdims=True) * (1.0 / width)
    centred = values - row_mean
    row_var = jnp.sum(centred * centred, axis=-1, keepdims=True) * (1.0 / width)
    scaled = centred * lax.rsqrt(row_var + norm_epsilon) * gain.astype(jnp.float32)
    return (scaled + bias.astype(jnp.float32)).astype(jnp.bfloat16)


def fill_normed(src_ref, gain, bias, dst_ref, first, count, base):
    def fill(i, carry):
        src = pl.multiple_of(first + i * NORM_ROWS, NORM_ROWS)
        dst = pl.multiple_of(base + first + i * NORM_ROWS, NORM_ROWS)
        dst_ref[pl.ds(dst, NORM_ROWS), :] = normalised(
            src_ref[pl.ds(src, NORM_ROWS), :], gain, bias
        )
        return carry

    lax.fori_loop(0, count // NORM_ROWS, fill, 0)


NORM_PARTS = 4


def norm_own_body(rows_hbm, gain_hbm, bias_hbm, out_ref, rows_ref, gain_ref, bias_ref, sems):
    count, width = rows_ref.shape
    part = count // NORM_PARTS
    small = [
        pltpu.make_async_copy(gain_hbm, gain_ref, sems.at[NORM_PARTS]),
        pltpu.make_async_copy(bias_hbm, bias_ref, sems.at[NORM_PARTS + 1]),
    ]
    parts = [
        pltpu.make_async_copy(
            rows_hbm.at[pl.ds(n * part, part)], rows_ref.at[pl.ds(n * part, part)], sems.at[n]
        )
        for n in range(NORM_PARTS)
    ]
    for copy in small + parts:
        copy.start()
    for copy in small:
        copy.wait()
    gain = gain_ref[...].reshape(1, width)
    bias = bias_ref[...].reshape(1, width)
    for n in range(NORM_PARTS):
        parts[n].wait()
        fill_normed(rows_ref, gain, bias, out_ref, n * part, part, 0)


def norm_own(rows, gain, bias):
    count, width = rows.shape
    return pl.pallas_call(
        norm_own_body,
        in_specs=[FAR_MEMORY] * 3,
        out_specs=WHOLE,
        out_shape=jax.ShapeDtypeStruct((count, width), jnp.bfloat16),
        scratch_shapes=[
            pltpu.VMEM((count, width), jnp.bfloat16),
            pltpu.VMEM((width,), jnp.bfloat16),
            pltpu.VMEM((width,), jnp.bfloat16),
            pltpu.SemaphoreType.DMA((NORM_PARTS + 2,)),
        ],
        compiler_params=limit(8),
        cost_estimate=pl.CostEstimate(
            flops=8_000_000_000, bytes_accessed=4 * count * width, transcendentals=0
        ),
        name="norm_own",
    )(rows, gain, bias)


def norm_other_body(own_ref, other_ref, gain_ref, bias_ref, out_ref):
    half, width = own_ref.shape
    core = lax.axis_index("mp")
    out_ref[pl.ds(pl.multiple_of(core * half, half), half), :] = own_ref[...]
    fill_normed(
        other_ref, gain_ref[...].reshape(1, width), bias_ref[...].reshape(1, width), out_ref,
        0, half, pl.multiple_of((1 - core) * half, half),
    )


def norm_other(own, other, gain, bias):
    half, width = own.shape
    return pl.pallas_call(
        norm_other_body,
        in_specs=[WHOLE] * 4,
        out_specs=WHOLE,
        out_shape=jax.ShapeDtypeStruct((2 * half, width), jnp.bfloat16),
        compiler_params=limit(6),
        cost_estimate=pl.CostEstimate(
            flops=10 * half * width, bytes_accessed=4 * half * width, transcendentals=0
        ),
        name="norm_other",
    )(own, other, gain, bias)


def project_body(
    counts_ref, shift_ref, normed_ref, w_ref, add_ref, rms_ref,
    out_ref, add_row, rms_row, squares, acc_even, acc_odd,
):
    rows = normed_ref.shape[0]
    columns = w_ref.shape[1]
    blocks = columns // COLUMNS
    total = image_starts(counts_ref, shift_ref)[1]
    mine = pl.multiple_of(lax.axis_index("mp") * columns, columns)
    add_row[...] = add_ref[...].reshape(1, columns).astype(jnp.float32)
    rms_row[...] = rms_ref[...].reshape(1, 2 * columns).astype(jnp.float32)
    acc_odd[...] = jnp.zeros_like(acc_odd)

    def run(bound):
        used = pl.ds(0, bound)

        def product(block, acc):
            at = pl.multiple_of(block * COLUMNS, COLUMNS)
            acc[used, :] = jnp.dot(
                normed_ref[used, :], w_ref[:, pl.ds(at, COLUMNS)],
                preferred_element_type=jnp.float32,
            )

        def post(block, acc, keep=None):
            at = pl.multiple_of(block * COLUMNS, COLUMNS)
            pre = acc[used, :] + add_row[:, pl.ds(at, COLUMNS)]
            value = pre * (1.0 + lax.erf(pre * np.float32(0.5**0.5))) * 0.5
            value = value.astype(jnp.bfloat16).astype(jnp.float32)
            gain = rms_row[:, pl.ds(pl.multiple_of(mine + at, COLUMNS), COLUMNS)]
            out_ref[used, pl.ds(at, COLUMNS)] = (value * gain).astype(jnp.bfloat16)
            square = value[:, :128] * value[:, :128] + value[:, 128:] * value[:, 128:]
            if keep is not None:
                square = jnp.where(keep, square, 0.0)
            squares[used, :] = squares[used, :] + square

        squares[...] = jnp.zeros_like(squares)

        def pair(p, carry):
            product(2 * p, acc_even)
            post(jnp.maximum(2 * p - 1, 0), acc_odd, p > 0)
            product(2 * p + 1, acc_odd)
            post(2 * p, acc_even)
            return carry

        lax.fori_loop(0, blocks // 2, pair, 0)
        post(blocks - 1, acc_odd)
        row_sum = jnp.sum(squares[used, :], axis=-1, keepdims=True)
        high = row_sum.astype(jnp.bfloat16).astype(jnp.float32)
        lane = lax.broadcasted_iota(jnp.int32, (bound, 128), 1)
        out_ref[used, columns : columns + 128] = jnp.where(
            lane < 64, high, row_sum - high
        ).astype(jnp.bfloat16)

    for_row_bound(total, rows, run)


def project(counts, shift, normed, w_proj, proj_bias, rms_gain):
    rows, width = normed.shape
    columns = w_proj.shape[1]
    return pl.pallas_call(
        project_body,
        in_specs=[SCALARS] * 2 + [WHOLE] * 4,
        out_specs=WHOLE,
        scratch_shapes=[
            pltpu.VMEM((1, columns), jnp.float32),
            pltpu.VMEM((1, 2 * columns), jnp.float32),
            pltpu.VMEM((rows, 128), jnp.float32),
            pltpu.VMEM((rows, COLUMNS), jnp.float32),
            pltpu.VMEM((rows, COLUMNS), jnp.float32),
        ],
        out_shape=jax.ShapeDtypeStruct((rows, columns + 128), jnp.bfloat16),
        compiler_params=limit(8),
        cost_estimate=pl.CostEstimate(
            flops=2 * rows * width * columns,
            bytes_accessed=2 * width * columns,
            transcendentals=rows * columns,
        ),
        name="project",
    )(counts, shift, normed, w_proj, proj_bias, rms_gain)


def first_half_body(counts_ref, shift_ref, gained_ref, w_ref, part_ref):
    rows = gained_ref.shape[0]
    depth = w_ref.shape[0] // 2
    mine = pl.multiple_of(lax.axis_index("mp") * depth, depth)
    total = image_starts(counts_ref, shift_ref)[1]

    def run(bound):
        def block(j, carry):
            at = pl.multiple_of(j * COLUMNS, COLUMNS)
            part_ref[pl.ds(0, bound), pl.ds(at, COLUMNS)] = jnp.dot(
                gained_ref[pl.ds(0, bound), pl.ds(0, depth)],
                w_ref[pl.ds(mine, depth), pl.ds(at, COLUMNS)],
                preferred_element_type=jnp.float32,
            )
            return carry

        lax.fori_loop(0, w_ref.shape[1] // COLUMNS, block, 0)

    for_row_bound(total, rows, run)


def first_half(counts, shift, gained, w_qkv):
    rows = gained.shape[0]
    depth, columns = w_qkv.shape
    return pl.pallas_call(
        first_half_body,
        in_specs=[SCALARS] * 2 + [WHOLE] * 2,
        out_specs=WHOLE,
        out_shape=jax.ShapeDtypeStruct((rows, columns), jnp.float32),
        compiler_params=limit(6),
        cost_estimate=pl.CostEstimate(
            flops=rows * depth * columns,
            bytes_accessed=depth * columns + 4 * rows * columns,
            transcendentals=0,
        ),
        name="first_half",
    )(counts, shift, gained, w_qkv)


def attend_body(
    counts_ref, shift_ref, near_ref, far_ref, w_ref, part_ref, cos_ref, sine_ref,
    out_ref, align, factor, turned_rows, slots, *heads,
):
    rows = far_ref.shape[0]
    depth = w_ref.shape[0] // 2
    senders = out_ref.shape[0]
    per_tile = TILE // IMG_MAX
    width = heads[0].shape[1]
    me = lax.axis_index("dp")
    far = pl.multiple_of((1 - lax.axis_index("mp")) * depth, depth)
    starts, total = image_starts(counts_ref, shift_ref)
    column = lax.broadcasted_iota(jnp.int32, (IMG_MAX, rows), 1)
    distance = column - lax.broadcasted_iota(jnp.int32, (IMG_MAX, rows), 0)
    for k, start in enumerate(starts):
        align[k * IMG_MAX : (k + 1) * IMG_MAX, :] = jnp.where(distance == start, 1.0, 0.0).astype(
            jnp.bfloat16
        )
    q_at = lax.broadcasted_iota(jnp.int32, (QUERY_PER_KEY * TILE, TILE), 0)
    k_at = lax.broadcasted_iota(jnp.int32, (QUERY_PER_KEY * TILE, TILE), 1)
    q_at = jnp.bitwise_and(q_at, TILE - 1)
    allowed = (q_at >= k_at) & ((q_at // IMG_MAX) == (k_at // IMG_MAX))

    def run(bound):
        used = slice(0, bound)
        both = near_ref[used, depth:].astype(jnp.float32) + far_ref[used, depth:].astype(
            jnp.float32
        )
        squares = both[:, 0:1] + both[:, 64:65]
        factor[used, :] = jnp.broadcast_to(
            lax.rsqrt(squares * (1.0 / (2 * depth)) + rms_epsilon), (bound, HEAD_SIZE)
        )

        def product(group):
            at = slice(group * width, (group + 1) * width)
            heads[group][used, :] = part_ref[used, at] + jnp.dot(
                far_ref[used, 0:depth], w_ref[pl.ds(far, depth), at],
                preferred_element_type=jnp.float32,
            )

        def attention(group):
            for n in range(QUERY_PER_KEY + 2):
                at = slice(n * HEAD_SIZE, (n + 1) * HEAD_SIZE)
                values = heads[group][used, at] * factor[used, :]
                if n <= QUERY_PER_KEY:
                    turned = pltpu.roll(values, HEAD_SIZE // 2, 1)
                    values = values * cos_ref[used, :] + turned * sine_ref[used, :]
                turned_rows[used, at] = values.astype(jnp.bfloat16)
            slots[...] = jnp.dot(
                align[:, used], turned_rows[used, :], preferred_element_type=jnp.float32
            ).astype(jnp.bfloat16)
            for tile in range(rows // TILE):
                at = slice(tile * TILE, (tile + 1) * TILE)

                def head(n):
                    return slots[at, n * HEAD_SIZE : (n + 1) * HEAD_SIZE]

                queries = jnp.concatenate([head(n) for n in range(QUERY_PER_KEY)], axis=0)
                scores = lax.dot_general(
                    queries, head(QUERY_PER_KEY), (((1,), (1,)), ((), ())),
                    preferred_element_type=jnp.float32,
                )
                scores = jnp.where(allowed, scores * np.float32(HEAD_SIZE**-0.5), -1e30)
                weights = jnp.exp(scores - jnp.max(scores, axis=-1, keepdims=True))
                inverse = 1.0 / jnp.sum(weights, axis=-1, keepdims=True)
                attended = jnp.dot(
                    (weights * inverse).astype(jnp.bfloat16), head(QUERY_PER_KEY + 1),
                    preferred_element_type=jnp.float32,
                ).astype(jnp.bfloat16)
                for j in range(per_tile):
                    target = lax.rem(me - shift_ref[tile * per_tile + j] + senders, senders)
                    for n in range(QUERY_PER_KEY):
                        column = (group * QUERY_PER_KEY + n) * HEAD_SIZE
                        out_ref[target, :, column : column + HEAD_SIZE] = attended[
                            n * TILE + j * IMG_MAX : n * TILE + (j + 1) * IMG_MAX, :
                        ]

        product(0)
        for group in range(1, len(heads)):
            product(group)
            attention(group - 1)
        attention(len(heads) - 1)

    for_row_bound(total, rows, run)


def attend(counts, shift, near, far, w_qkv, part, senders):
    rows = far.shape[0]
    block = (QUERY_PER_KEY + 2) * HEAD_SIZE
    depth, columns = w_qkv.shape
    groups = columns // block
    out_columns = groups * QUERY_PER_KEY * HEAD_SIZE
    cos, sine = rotary_tables(rows)
    return pl.pallas_call(
        attend_body,
        in_specs=[SCALARS] * 2 + [WHOLE] * 6,
        out_specs=WHOLE,
        scratch_shapes=[
            pltpu.VMEM((rows, rows), jnp.bfloat16),
            pltpu.VMEM((rows, HEAD_SIZE), jnp.float32),
            pltpu.VMEM((rows, block), jnp.bfloat16),
            pltpu.VMEM((rows, block), jnp.bfloat16),
        ]
        + [pltpu.VMEM((rows, block), jnp.float32)] * groups,
        out_shape=jax.ShapeDtypeStruct((senders, IMG_MAX, out_columns), jnp.bfloat16),
        compiler_params=limit(12),
        cost_estimate=pl.CostEstimate(
            flops=rows * depth * columns, bytes_accessed=depth * columns, transcendentals=0
        ),
        name="attend",
    )(counts, shift, near, far, w_qkv, part, cos, sine)


def place_body(counts_ref, shift_ref, box_ref, out_hbm, placed, sems):
    senders = box_ref.shape[0]
    per_tile = counts_ref.shape[0]
    tiles = shift_ref.shape[0] // per_tile
    me = lax.axis_index("dp")
    lane = lax.broadcasted_iota(jnp.int32, (TILE, TILE), 1)
    row = lax.broadcasted_iota(jnp.int32, (TILE, TILE), 0)
    inside = jnp.bitwise_and(lane, IMG_MAX - 1)
    image = lane // IMG_MAX
    copies = []
    for tile in range(tiles):
        goal = jnp.full((TILE, TILE), -1, jnp.int32)
        offset = jnp.int32(0)
        blocks = []
        for j in range(per_tile):
            count = counts_ref[j, me * tiles + tile]
            goal = jnp.where((image == j) & (inside < count), inside + offset, goal)
            offset = offset + count
            source = lax.rem(me + shift_ref[tile * per_tile + j], senders)
            blocks.append(box_ref[source])
        at = pl.ds(tile * TILE, TILE)
        placed[at, :] = jnp.dot(
            jnp.where(row == goal, 1.0, 0.0).astype(jnp.bfloat16),
            jnp.concatenate(blocks, axis=0),
            preferred_element_type=jnp.float32,
        ).astype(jnp.bfloat16)
        copy = pltpu.make_async_copy(placed.at[at], out_hbm.at[at], sems.at[tile])
        copy.start()
        copies.append(copy)
    for copy in copies:
        copy.wait()


def place_rows(counts, shift, box):
    senders, depth, columns = box.shape
    rows = shift.shape[0] * depth
    return pl.pallas_call(
        place_body,
        in_specs=[SCALARS] * 2 + [WHOLE],
        out_specs=FAR_MEMORY,
        out_shape=jax.ShapeDtypeStruct((rows, columns), jnp.bfloat16),
        scratch_shapes=[
            pltpu.VMEM((rows, columns), jnp.bfloat16),
            pltpu.SemaphoreType.DMA((rows // TILE,)),
        ],
        compiler_params=limit(8),
        name="place_rows",
    )(counts, shift, box)


def local(
    patches, ln_gain, ln_bias, w_proj, proj_bias, rms_gain, w_qkv, image_counts, source_shift
):
    senders = lax.axis_size("dp")
    counts = image_counts.T
    other = lax.ppermute(patches, "mp", SWAP)
    pin = lambda x: pltpu.with_memory_space_constraint(x, pltpu.HBM)
    own = norm_own(pin(patches), pin(ln_gain), pin(ln_bias))
    normed = norm_other(own, other, ln_gain, ln_bias)
    near = project(counts, source_shift, normed, w_proj, proj_bias, rms_gain)
    far = lax.ppermute(near, "mp", SWAP)
    part = first_half(counts, source_shift, near, w_qkv)
    outbox = attend(counts, source_shift, near, far, w_qkv, part, senders)
    in_box = lax.all_to_all(outbox, "dp", split_axis=0, concat_axis=0, tiled=True)
    return place_rows(counts, source_shift, in_box)


def solution(mesh):
    in_specs = (
        P(("dp", "mp"), None),
        P(),
        P(),
        P(None, "mp"),
        P("mp"),
        P(),
        P(None, "mp"),
        P(),
        P(),
    )
    out_specs = P("dp", "mp")
    return jax.shard_map(local, mesh=mesh, in_specs=in_specs, out_specs=out_specs, check_vma=False)
```

time: 76.7 us -> 68.9 us (0.90)
  local copies, waits for them, and re-layouts: 5.83 us -> 0.07 us
  Pallas kernels: 28.3 us -> 26 us
    unnamed x28 -> x24, local copies, waits for them, and re-layouts: 5.13 us -> 0.07 us
    pallas_call x5 -> x6, Pallas kernels: 28.3 us -> 26 us  [the longest x1 7.19 us: project(): pl.pallas_call(project_body, in_specs=[SCALARS] * 2 + [WHOLE] * 4, out_sp...]
  transfers between devices with their start and end apart: 2 -> 2, of which waited for: 0 -> 1; matrix products, arithmetic and copies ran while one was open for 1% -> 0% of each run, Pallas kernels for 10% -> 11%
where the time goes in v3:
time: 68.9 us; the launch traced here: 68.8 us
  blocking collectives  41.7 us (61%)
  Pallas kernels  26 us (38%)
    all_to_all x1, blocking collectives, local(): lax.all_to_all(outbox, 'dp', split_axis=0, concat_axis=0, tiled=True)  41.7 us
    pallas_call x1, Pallas kernels, project(): pl.pallas_call(project_body, in_specs=[SCALARS] * 2 + [WHOLE] * 4, out_sp...  7.19 us
    pallas_call x1, Pallas kernels, attend(): pl.pallas_call(attend_body, in_specs=[SCALARS] * 2 + [WHOLE] * 6, out_spe...  6.74 us
    pallas_call x1, Pallas kernels, first_half(): pl.pallas_call(first_half_body, in_specs=[SCALARS] * 2 + [WHOLE] * 2, out...  4.13 us
    pallas_call x1, Pallas kernels, norm_own(): pl.pallas_call(norm_own_body, in_specs=[FAR_MEMORY] * 3, out_specs=WHOLE,...  3.49 us
    pallas_call x1, Pallas kernels, norm_other(): pl.pallas_call(norm_other_body, in_specs=[WHOLE] * 4, out_specs=WHOLE, ou...  2.55 us
    pallas_call x1, Pallas kernels, place_rows(): pl.pallas_call(place_body, in_specs=[SCALARS] * 2 + [WHOLE], out_specs=FA...  1.91 us
  transfers between devices with their start and end apart: 2, of which 1 were waited for; matrix products, arithmetic and copies ran while one was open for 0% of the time, Pallas kernels for 11%

profile of v3, /device:TPU:0, one launch (start us, length us, event | category | flops | bytes accessed | tf_op | source)
XLA Modules:
  0.0 68.8 jit_solution(12476110575332052766)
XLA Ops:
  0.0 0.0 copy-start.4
  0.0 0.0 copy-start.3
  0.0 0.0 collective-permute-start
  0.0 0.0 copy-start.6
  0.0 3.5 %norm_own.1.own_ref = bf16[256,3200]{1,0:T(8,128)(2,1)S(1)} custom-call(bf16[256,3200]{1,0:T(8,128)(2,1)} %rows_hbm.1, bf16[3200]{0:T(1024)(128)(2,1)} %gain_ref.1, bf16[3200]{0:T(1024)(128)(2,1)} %bias_ref.1), custom_call_target="tpu_custom_call" | custom-call | flops 8000000000 | bytes 3276800 | tf_op jit(solution)/shard_map/norm_own/pallas_call | solution.py:117
  3.5 0.0 copy-start.2
  3.5 0.0 copy-start.5
  3.5 0.0 copy-start.7
  3.5 0.0 copy-start.8
  3.6 0.2 collective-permute-done.other_ref
  3.7 0.0 copy-done.4
  3.7 0.0 copy-done.3
  3.7 0.0 slice-start
  3.7 2.6 %norm_other.1.normed_ref = bf16[512,3200]{1,0:T(8,128)(2,1)S(1)} custom-call(bf16[256,3200]{1,0:T(8,128)(2,1)S(1)} %norm_own.1.own_ref, bf16[256,3200]{1,0:T(8,128)(2,1)S(1)} %collective-permute-done.other_ref, bf16[3200]{0:T(1024)(128)(2,1)S(1)} %copy-done.3, bf16[3200]{0:T(1024)(128)(2,1)S(1)} %copy-done.4), custom_call_target="tpu_custom_call" | custom-call | flops 8192000 | bytes 3276800 | tf_op jit(solution)/shard_map/norm_other/pallas_call | solution.py:148
  6.3 0.0 copy-done.6
  6.3 0.0 copy-done.2
  6.3 0.0 copy-done.5
  6.3 0.0 copy-done.7
  6.3 0.0 copy-done.8
  6.3 0.0 slice-start.1
  6.3 0.0 slice-start.2
  6.4 7.2 %project.1.gained_ref.near_ref = bf16[512,2176]{1,0:T(8,128)(2,1)S(1)} custom-call(s32[8,256]{1,0:T(8,128)S(1)} %bitcast.3, s32[32]{0:T(128)S(1)} %copy-done.5, bf16[512,3200]{1,0:T(8,128)(2,1)S(1)} %norm_other.1.normed_ref, bf16[3200,2048]{1,0:T(8,128)(2,1)S(1)} %copy-done.6, bf16[2048]{0:T(1024)(128)(2,1)S(1)} %copy-done.8, bf16[4096]{0:T(1024)(128)(2,1)S(1)} %copy-done.7), custom_call_target="tpu_custom_call" | custom-call | flops 6710886400 | bytes 13107200 | tf_op jit(solution)/shard_map/project/pallas_call | solution.py:220
  13.6 0.0 copy-start
  13.6 0.0 copy-start.1
  13.6 0.5 collective-permute-start.1
  14.1 0.0 slice-done
  14.1 0.0 slice-done.1
  14.1 0.0 slice-done.2
  14.1 4.1 %first_half.1.part_ref = f32[512,1536]{1,0:T(8,128)S(1)} custom-call(s32[8,256]{1,0:T(8,128)S(1)} %bitcast.4, s32[32]{0:T(128)S(1)} %copy-done.5, bf16[512,2176]{1,0:T(8,128)(2,1)S(1)} %project.1.gained_ref.near_ref, bf16[4096,1536]{1,0:T(8,128)(2,1)S(1)} %bitcast.2), custom_call_target="tpu_custom_call" | custom-call | flops 3221225472 | bytes 9437184 | tf_op jit(solution)/shard_map/first_half/pallas_call | solution.py:266
  18.2 0.0 collective-permute-done.1.far_ref
  18.2 0.0 copy-done
  18.2 0.0 copy-done.1
  18.2 6.7 %attend.1 = bf16[64,16,1024]{2,1,0:T(8,128)(2,1)S(1)} custom-call(s32[8,256]{1,0:T(8,128)S(1)} %bitcast.5, s32[32]{0:T(128)S(1)} %copy-done.5, bf16[512,2176]{1,0:T(8,128)(2,1)S(1)} %project.1.gained_ref.near_ref, bf16[512,2176]{1,0:T(8,128)(2,1)S(1)} %collective-permute-done.1.far_ref, bf16[4096,1536]{1,0:T(8,128)(2,1)S(1)} %bitcast.2, ...), custom_call_target="tpu_custom_call" | custom-call | flops 3221225472 | bytes 6291456 | tf_op jit(solution)/shard_map/attend/pallas_call | solution.py:374
  25.0 41.7 %all_to_all.5.box_ref = bf16[64,16,1024]{2,1,0:T(8,128)(2,1)S(1)} all-to-all(bf16[64,16,1024]{2,1,0:T(8,128)(2,1)S(1)} %attend.1), channel_id=1, replica_groups=mesh['dp'=64,'mp'=2] {'dp'}, dimensions={0} | all-to-all | bytes 4194304 | tf_op jit(solution)/shard_map/all_to_all | solution.py:457
  66.7 1.9 %place_rows.1 = bf16[512,1024]{1,0:T(8,128)(2,1)} custom-call(s32[8,256]{1,0:T(8,128)S(1)} %bitcast.6, s32[32]{0:T(128)S(1)} %copy-done.5, bf16[64,16,1024]{2,1,0:T(8,128)(2,1)S(1)} %all_to_all.5.box_ref), custom_call_target="tpu_custom_call" | custom-call | tf_op jit(solution)/shard_map/place_rows/pallas_call | solution.py:430
  (1 shorter events, 0.0 us)
Async XLA Ops:
  0.0 3.7 %copy-start.4 = (bf16[3200]{0:T(1024)(128)(2,1)S(1)}, bf16[3200]{0:T(1024)(128)(2,1)}, u32[]{:S(2)}) copy-start(bf16[3200]{0:T(1024)(128)(2,1)} %bias_ref.1) | copy-start | bytes 19204
  0.0 3.7 %copy-start.3 = (bf16[3200]{0:T(1024)(128)(2,1)S(1)}, bf16[3200]{0:T(1024)(128)(2,1)}, u32[]{:S(2)}) copy-start(bf16[3200]{0:T(1024)(128)(2,1)} %gain_ref.1) | copy-start | bytes 19204
  0.0 3.7 %collective-permute-start = (bf16[256,3200]{1,0:T(8,128)(2,1)}, bf16[256,3200]{1,0:T(8,128)(2,1)S(1)}, u32[]{:S(2)}, u32[]{:S(2)}) collective-permute-start(bf16[256,3200]{1,0:T(8,128)(2,1)} %rows_hbm.1), channel_id=1, source_target_pairs={{0,1},{1,0},{2,3},{3,2},{4,5},{5,4},{6,7},{7,6},{8,9},{9,8},{10,11... | collective-permute-start | bytes 4915208 | tf_op jit(solution)/shard_map/ppermute | solution.py:449
  0.0 6.3 %copy-start.6 = (bf16[3200,2048]{1,0:T(8,128)(2,1)S(1)}, bf16[3200,2048]{1,0:T(8,128)(2,1)}, u32[]{:S(2)}) copy-start(bf16[3200,2048]{1,0:T(8,128)(2,1)} %w_ref.3) | copy-start | bytes 39321604
  3.5 2.8 %copy-start.2 = (s32[256,8]{0,1:T(8,128)S(1)}, s32[256,8]{0,1:T(8,128)}, u32[]{:S(2)}) copy-start(s32[256,8]{0,1:T(8,128)} %param.18) | copy-start | bytes 24580
  3.5 2.8 %copy-start.5 = (s32[32]{0:T(128)S(1)}, s32[32]{0:T(128)}, u32[]{:S(2)}) copy-start(s32[32]{0:T(128)} %shift_ref.7) | copy-start | bytes 388
  3.5 2.8 %copy-start.7 = (bf16[4096]{0:T(1024)(128)(2,1)S(1)}, bf16[4096]{0:T(1024)(128)(2,1)}, u32[]{:S(2)}) copy-start(bf16[4096]{0:T(1024)(128)(2,1)} %rms_ref.1) | copy-start | bytes 24580
  3.5 2.8 %copy-start.8 = (bf16[2048]{0:T(1024)(128)(2,1)S(1)}, bf16[2048]{0:T(1024)(128)(2,1)}, u32[]{:S(2)}) copy-start(bf16[2048]{0:T(1024)(128)(2,1)} %add_ref.1) | copy-start | bytes 12292
  3.7 10.3 %slice-start = ((s8[12582912]{0:T(1024)(128)(4,1)}), s8[4194304]{0:T(1024)(128)(4,1)S(1)}, s32[]{:S(2)}) async-start(s8[12582912]{0:T(1024)(128)(4,1)} %bitcast.1), calls=%async_computation.1 | async-start | bytes 8388608
  6.3 7.7 %slice-start.1 = ((s8[12582912]{0:T(1024)(128)(4,1)}), s8[4194304]{0:T(1024)(128)(4,1)S(1)}, s32[]{:S(2)}) async-start(s8[12582912]{0:T(1024)(128)(4,1)} %bitcast.1), calls=%async_computation.2 | async-start | bytes 8388608
  6.3 7.7 %slice-start.2 = ((s8[12582912]{0:T(1024)(128)(4,1)}), s8[4194304]{0:T(1024)(128)(4,1)S(1)}, s32[]{:S(2)}) async-start(s8[12582912]{0:T(1024)(128)(4,1)} %bitcast.1), calls=%async_computation.3 | async-start | bytes 8388608
  13.6 4.7 %copy-start = (f32[512,128]{1,0:T(8,128)S(1)}, f32[512,128]{1,0:T(8,128)}, u32[]{:S(2)}) copy-start(f32[512,128]{1,0:T(8,128)} %constant.5.clone.sine_ref) | copy-start | bytes 786436
  13.6 4.7 %copy-start.1 = (f32[512,128]{1,0:T(8,128)S(1)}, f32[512,128]{1,0:T(8,128)}, u32[]{:S(2)}) copy-start(f32[512,128]{1,0:T(8,128)} %constant.4.clone.cos_ref) | copy-start | bytes 786436
  13.6 4.6 %collective-permute-start.1 = (bf16[512,2176]{1,0:T(8,128)(2,1)S(1)}, bf16[512,2176]{1,0:T(8,128)(2,1)S(1)}, u32[]{:S(2)}, u32[]{:S(2)}) collective-permute-start(bf16[512,2176]{1,0:T(8,128)(2,1)S(1)} %project.1.gained_ref.near_ref), channel_id=1, source_target_pairs={{0,1},{1,0},{2,3},{3,2},{4,5},{5,4},{6,7},{7,6},{8,9},{9,8},{10,11... | collective-permute-start | bytes 6684680 | tf_op jit(solution)/shard_map/ppermute | solution.py:454

commit v4 on v3

v4 whole, which is shorter than its diff:
```python
import functools

import jax
import jax.numpy as jnp
import numpy as np
from jax import lax
from jax.experimental import pallas as pl
from jax.experimental.pallas import tpu as pltpu
from jax.sharding import PartitionSpec as P

HEAD_SIZE = 128
TILE = 128
QUERY_PER_KEY = 4
IMG_MAX = 16

norm_epsilon = 1e-05
rms_epsilon = 1e-05
rotary_base = 500000.0

SWAP = [(0, 1), (1, 0)]


WHOLE = pl.BlockSpec(memory_space=pltpu.VMEM)
SCALARS = pl.BlockSpec(memory_space=pltpu.SMEM)
FAR_MEMORY = pl.BlockSpec(memory_space=pltpu.HBM)
NORM_ROWS = 32
CUTS = (1024, 768, 256)
NARROW = 256
QKV_COLUMNS = 768
WINDOW = TILE + 2 * IMG_MAX
ROW_BOUNDS = (352, 384)


def limit(mib):
    return pltpu.CompilerParams(vmem_limit_bytes=mib * 1024 * 1024)


def rotary_tables(rows):
    half = HEAD_SIZE // 2
    frequency = rotary_base ** (-(np.arange(half, dtype=np.float64) * (2.0 / HEAD_SIZE)))
    angles = np.arange(rows, dtype=np.float64)[:, None] * frequency[None, :]
    cos = np.concatenate([np.cos(angles), np.cos(angles)], axis=-1)
    sine = np.concatenate([-np.sin(angles), np.sin(angles)], axis=-1)
    return jnp.asarray(cos.astype(np.float32)), jnp.asarray(sine.astype(np.float32))


def write_plan(counts_ref, shift_ref, plan_ref):
    images = shift_ref.shape[0]
    tile_images = counts_ref.shape[0]
    tiles = images // tile_images
    senders = counts_ref.shape[1] // tiles
    me = lax.axis_index("dp")
    start = jnp.int32(0)
    for k in range(images):
        plan_ref[k] = start
        target = lax.rem(me - shift_ref[k] + senders, senders)
        plan_ref[images + 1 + k] = target
        start = start + counts_ref[k % tile_images, target * tiles + k // tile_images]
    plan_ref[images] = start


def for_row_bound(total, most, run):
    below = jnp.int32(-1)
    for bound in (*ROW_BOUNDS, most):
        pl.when((total > below) & (total <= bound))(functools.partial(run, bound))
        below = jnp.int32(bound)


def normalised(rows, gain, bias):
    values = rows.astype(jnp.float32)
    width = values.shape[-1]
    row_mean = jnp.sum(values, axis=-1, keepdims=True) * (1.0 / width)
    centred = values - row_mean
    row_var = jnp.sum(centred * centred, axis=-1, keepdims=True) * (1.0 / width)
    scaled = centred * lax.rsqrt(row_var + norm_epsilon) * gain
    return (scaled + bias).astype(jnp.bfloat16)


def fill_normed(src_ref, gain_row, bias_row, dst_ref, first, count, base):
    def fill(i, carry):
        src = pl.multiple_of(first + i * NORM_ROWS, NORM_ROWS)
        dst = pl.multiple_of(base + first + i * NORM_ROWS, NORM_ROWS)
        dst_ref[pl.ds(dst, NORM_ROWS), :] = normalised(
            src_ref[pl.ds(src, NORM_ROWS), :], gain_row[...], bias_row[...]
        )
        return carry

    lax.fori_loop(0, count // NORM_ROWS, fill, 0, unroll=2)


NORM_PARTS = 4


def norm_own_body(rows_hbm, gain_hbm, bias_hbm, out_ref, rows_ref, gain_ref, bias_ref, gain_row, bias_row, sems):
    count, width = rows_ref.shape
    part = count // NORM_PARTS
    small = [
        pltpu.make_async_copy(gain_hbm, gain_ref, sems.at[NORM_PARTS]),
        pltpu.make_async_copy(bias_hbm, bias_ref, sems.at[NORM_PARTS + 1]),
    ]
    parts = [
        pltpu.make_async_copy(
            rows_hbm.at[pl.ds(n * part, part)], rows_ref.at[pl.ds(n * part, part)], sems.at[n]
        )
        for n in range(NORM_PARTS)
    ]
    for copy in small + parts:
        copy.start()
    for copy in small:
        copy.wait()
    gain_row[...] = gain_ref[...].reshape(1, width).astype(jnp.float32)
    bias_row[...] = bias_ref[...].reshape(1, width).astype(jnp.float32)
    for n in range(NORM_PARTS):
        parts[n].wait()
        fill_normed(rows_ref, gain_row, bias_row, out_ref, n * part, part, 0)


def norm_own(rows, gain, bias):
    count, width = rows.shape
    return pl.pallas_call(
        norm_own_body,
        in_specs=[FAR_MEMORY] * 3,
        out_specs=WHOLE,
        out_shape=jax.ShapeDtypeStruct((count, width), jnp.bfloat16),
        scratch_shapes=[
            pltpu.VMEM((count, width), jnp.bfloat16),
            pltpu.VMEM((width,), jnp.bfloat16),
            pltpu.VMEM((width,), jnp.bfloat16),
            pltpu.VMEM((1, width), jnp.float32),
            pltpu.VMEM((1, width), jnp.float32),
            pltpu.SemaphoreType.DMA((NORM_PARTS + 2,)),
        ],
        compiler_params=limit(8),
        cost_estimate=pl.CostEstimate(
            flops=8_000_000_000, bytes_accessed=4 * count * width, transcendentals=0
        ),
        name="norm_own",
    )(rows, gain, bias)


def norm_other_body(
    counts_ref, shift_ref, own_ref, other_ref, gain_ref, bias_ref, out_ref, plan_ref,
    gain_row, bias_row,
):
    write_plan(counts_ref, shift_ref, plan_ref)
    half, width = own_ref.shape
    core = lax.axis_index("mp")
    out_ref[pl.ds(pl.multiple_of(core * half, half), half), :] = own_ref[...]
    gain_row[...] = gain_ref[...].reshape(1, width).astype(jnp.float32)
    bias_row[...] = bias_ref[...].reshape(1, width).astype(jnp.float32)
    fill_normed(
        other_ref, gain_row, bias_row, out_ref, 0, half, pl.multiple_of((1 - core) * half, half)
    )


def norm_other(counts, shift, own, other, gain, bias):
    half, width = own.shape
    images = shift.shape[0]
    return pl.pallas_call(
        norm_other_body,
        in_specs=[SCALARS] * 2 + [WHOLE] * 4,
        out_specs=[WHOLE, SCALARS],
        out_shape=[
            jax.ShapeDtypeStruct((2 * half, width), jnp.bfloat16),
            jax.ShapeDtypeStruct((2 * images + 1,), jnp.int32),
        ],
        scratch_shapes=[pltpu.VMEM((1, width), jnp.float32)] * 2,
        compiler_params=limit(6),
        cost_estimate=pl.CostEstimate(
            flops=10 * half * width, bytes_accessed=4 * half * width, transcendentals=0
        ),
        name="norm_other",
    )(counts, shift, own, other, gain, bias)


def project_body(
    plan_ref, normed_ref, w_ref, add_ref, rms_ref,
    out_ref, add_row, rms_row, squares, acc_even, acc_odd,
):
    rows = normed_ref.shape[0]
    columns = w_ref.shape[1]
    total = plan_ref[plan_ref.shape[0] // 2]
    mine = pl.multiple_of(lax.axis_index("mp") * columns, columns)
    add_row[...] = add_ref[...].reshape(1, columns).astype(jnp.float32)
    rms_row[...] = rms_ref[...].reshape(1, 2 * columns).astype(jnp.float32)

    def run(bound):
        used = pl.ds(0, bound)

        def product(first, width, acc):
            acc[used, 0:width] = jnp.dot(
                normed_ref[used, :], w_ref[:, pl.ds(first, width)],
                preferred_element_type=jnp.float32,
            )

        def post(first, width, acc):
            pre = acc[used, 0:width] + add_row[:, pl.ds(first, width)]
            value = pre * (1.0 + lax.erf(pre * np.float32(0.5**0.5))) * 0.5
            value = value.astype(jnp.bfloat16).astype(jnp.float32)
            gain = rms_row[:, pl.ds(pl.multiple_of(mine + first, NARROW), width)]
            out_ref[used, pl.ds(first, width)] = (value * gain).astype(jnp.bfloat16)
            square = sum(
                value[:, c : c + 128] * value[:, c : c + 128] for c in range(0, width, 128)
            )
            squares[used, :] = squares[used, :] + square

        squares[...] = jnp.zeros_like(squares)
        if bound < rows:
            first, waiting = 0, None
            for n, width in enumerate(CUTS):
                acc = (acc_even, acc_odd)[n % 2]
                product(first, width, acc)
                if waiting is not None:
                    post(*waiting)
                waiting = (first, width, acc)
                first += width
            post(*waiting)
        else:

            def block(n, carry):
                at = pl.multiple_of(n * NARROW, NARROW)
                product(at, NARROW, acc_even)
                post(at, NARROW, acc_even)
                return carry

            lax.fori_loop(0, columns // NARROW, block, 0)
        row_sum = jnp.sum(squares[used, :], axis=-1, keepdims=True)
        high = row_sum.astype(jnp.bfloat16).astype(jnp.float32)
        lane = lax.broadcasted_iota(jnp.int32, (bound, 128), 1)
        out_ref[used, columns : columns + 128] = jnp.where(
            lane < 64, high, row_sum - high
        ).astype(jnp.bfloat16)

    for_row_bound(total, rows, run)


def project(plan, normed, w_proj, proj_bias, rms_gain):
    rows, width = normed.shape
    columns = w_proj.shape[1]
    return pl.pallas_call(
        project_body,
        in_specs=[SCALARS] + [WHOLE] * 4,
        out_specs=WHOLE,
        scratch_shapes=[
            pltpu.VMEM((1, columns), jnp.float32),
            pltpu.VMEM((1, 2 * columns), jnp.float32),
            pltpu.VMEM((rows, 128), jnp.float32),
            pltpu.VMEM((rows, CUTS[0]), jnp.float32),
            pltpu.VMEM((rows, CUTS[1]), jnp.float32),
        ],
        out_shape=jax.ShapeDtypeStruct((rows, columns + 128), jnp.bfloat16),
        compiler_params=limit(18),
        cost_estimate=pl.CostEstimate(
            flops=2 * rows * width * columns,
            bytes_accessed=2 * width * columns,
            transcendentals=rows * columns,
        ),
        name="project",
    )(plan, normed, w_proj, proj_bias, rms_gain)


def first_half_body(plan_ref, gained_ref, w_ref, part_ref):
    rows = gained_ref.shape[0]
    depth = w_ref.shape[0] // 2
    mine = pl.multiple_of(lax.axis_index("mp") * depth, depth)
    total = plan_ref[plan_ref.shape[0] // 2]

    def run(bound):
        def block(j, carry):
            at = pl.multiple_of(j * QKV_COLUMNS, QKV_COLUMNS)
            part_ref[pl.ds(0, bound), pl.ds(at, QKV_COLUMNS)] = jnp.dot(
                gained_ref[pl.ds(0, bound), pl.ds(0, depth)],
                w_ref[pl.ds(mine, depth), pl.ds(at, QKV_COLUMNS)],
                preferred_element_type=jnp.float32,
            )
            return carry

        lax.fori_loop(0, w_ref.shape[1] // QKV_COLUMNS, block, 0)

    for_row_bound(total, rows, run)


def first_half(plan, gained, w_qkv):
    rows = gained.shape[0]
    depth, columns = w_qkv.shape
    return pl.pallas_call(
        first_half_body,
        in_specs=[SCALARS] + [WHOLE] * 2,
        out_specs=WHOLE,
        out_shape=jax.ShapeDtypeStruct((rows, columns), jnp.float32),
        compiler_params=limit(6),
        cost_estimate=pl.CostEstimate(
            flops=rows * depth * columns,
            bytes_accessed=depth * columns + 4 * rows * columns,
            transcendentals=0,
        ),
        name="first_half",
    )(plan, gained, w_qkv)


def attend_body(
    plan_ref, near_ref, far_ref, w_ref, part_ref, cos_ref, sine_ref,
    out_ref, factor, ones, align, heads, turned_rows, queries, keys, values, scores,
):
    groups, padded, width = turned_rows.shape
    rows = far_ref.shape[0]
    depth = w_ref.shape[0] // 2
    images = plan_ref.shape[0] // 2
    per_tile = TILE // IMG_MAX
    tiles = rows // TILE
    pair = 2 * HEAD_SIZE
    far = pl.multiple_of((1 - lax.axis_index("mp")) * depth, depth)
    starts = [plan_ref[k] for k in range(images)]
    total = plan_ref[images]
    targets = [plan_ref[images + 1 + k] for k in range(images)]
    bases = [
        pl.multiple_of((starts[tile * per_tile] // IMG_MAX) * IMG_MAX, IMG_MAX)
        for tile in range(tiles)
    ]

    def prepare():
        column = lax.broadcasted_iota(jnp.int32, (IMG_MAX, WINDOW), 1)
        distance = column - lax.broadcasted_iota(jnp.int32, (IMG_MAX, WINDOW), 0)
        empty = jnp.zeros((groups, tiles, HEAD_SIZE, HEAD_SIZE), jnp.bfloat16)
        for tile in range(tiles):
            for j in range(per_tile):
                align[tile, j * IMG_MAX : (j + 1) * IMG_MAX, :] = jnp.where(
                    distance == starts[tile * per_tile + j] - bases[tile], 1.0, 0.0
                ).astype(jnp.bfloat16)
        for kept in (keys, values):
            kept[:, :, 0:HEAD_SIZE, HEAD_SIZE:pair] = empty
            kept[:, :, HEAD_SIZE:pair, 0:HEAD_SIZE] = empty
        side = lax.broadcasted_iota(jnp.int32, (pair, pair), 0) // HEAD_SIZE
        ones[...] = jnp.where(
            side == lax.broadcasted_iota(jnp.int32, (pair, pair), 1) // HEAD_SIZE, 1.0, 0.0
        ).astype(jnp.bfloat16)

    q_at = jnp.bitwise_and(lax.broadcasted_iota(jnp.int32, (pair, pair), 0), TILE - 1)
    k_at = jnp.bitwise_and(lax.broadcasted_iota(jnp.int32, (pair, pair), 1), TILE - 1)
    allowed = (q_at >= k_at) & ((q_at // IMG_MAX) == (k_at // IMG_MAX))

    def line_up(group):
        for tile in range(tiles):
            window = turned_rows[group, pl.ds(bases[tile], WINDOW), :]
            placed = jnp.dot(align[tile], window, preferred_element_type=jnp.float32).astype(
                jnp.bfloat16
            )
            queries[group, tile * TILE : (tile + 1) * TILE, :] = placed[:, 0 : 2 * pair]
            for kept, n in ((keys, QUERY_PER_KEY), (values, QUERY_PER_KEY + 1)):
                block = placed[:, n * HEAD_SIZE : (n + 1) * HEAD_SIZE]
                kept[group, tile, 0:TILE, 0:HEAD_SIZE] = block
                kept[group, tile, TILE : 2 * TILE, HEAD_SIZE:pair] = block

    def score(group):
        for tile in range(tiles):
            at = slice(tile * TILE, (tile + 1) * TILE)
            stacked = jnp.concatenate(
                [queries[group, at, 0:pair], queries[group, at, pair : 2 * pair]], axis=0
            )
            scores[group, tile] = lax.dot_general(
                stacked, keys[group, tile], (((1,), (1,)), ((), ())),
                preferred_element_type=jnp.float32,
            )

    def weigh(group):
        for tile in range(tiles):
            seen = jnp.where(allowed, scores[group, tile] * np.float32(HEAD_SIZE**-0.5), -1e30)
            weights = jnp.concatenate(
                [
                    jnp.exp(half - jnp.max(half, axis=-1, keepdims=True)).astype(jnp.bfloat16)
                    for half in (seen[:, 0:HEAD_SIZE], seen[:, HEAD_SIZE:pair])
                ],
                axis=1,
            )
            weighed = jnp.dot(weights, values[group, tile], preferred_element_type=jnp.float32)
            row_sum = jnp.dot(weights, ones[...], preferred_element_type=jnp.float32)
            attended = (weighed * (1.0 / row_sum)).astype(jnp.bfloat16)
            for j in range(per_tile):
                target = targets[tile * per_tile + j]
                for n in range(2):
                    column = group * QUERY_PER_KEY * HEAD_SIZE + n * pair
                    out_ref[target, :, column : column + pair] = attended[
                        n * TILE + j * IMG_MAX : n * TILE + (j + 1) * IMG_MAX, :
                    ]

    def run(bound):
        used = slice(0, bound)
        both = near_ref[used, depth:].astype(jnp.float32) + far_ref[used, depth:].astype(
            jnp.float32
        )
        squares = both[:, 0:1] + both[:, 64:65]
        factor[used, :] = jnp.broadcast_to(
            lax.rsqrt(squares * (1.0 / (2 * depth)) + rms_epsilon), (bound, HEAD_SIZE)
        )

        def piece(group, first, size):
            at = pl.ds(group * width + first, size)
            heads[group, used, pl.ds(first, size)] = part_ref[used, at] + jnp.dot(
                far_ref[used, 0:depth], w_ref[pl.ds(far, depth), at],
                preferred_element_type=jnp.float32,
            )

        def product(group, first, last):
            if bound < rows:
                piece(group, first, last - first)
            else:

                def narrow(n, carry):
                    piece(group, pl.multiple_of(first + n * NARROW, NARROW), NARROW)
                    return carry

                lax.fori_loop(0, (last - first) // NARROW, narrow, 0)

        def rotate(group):
            for n in range(QUERY_PER_KEY + 2):
                at = slice(n * HEAD_SIZE, (n + 1) * HEAD_SIZE)
                rows_in = heads[group, used, at] * factor[used, :]
                if n <= QUERY_PER_KEY:
                    turned = pltpu.roll(rows_in, HEAD_SIZE // 2, 1)
                    rows_in = rows_in * cos_ref[used, :] + turned * sine_ref[used, :]
                turned_rows[group, used, at] = rows_in.astype(jnp.bfloat16)

        product(0, 0, width)
        prepare()
        turned_rows[:, bound:, :] = jnp.zeros((groups, padded - bound, width), jnp.bfloat16)
        for group in range(1, groups):
            product(group, 0, 512)
            rotate(group - 1)
            line_up(group - 1)
            score(group - 1)
            product(group, 512, width)
            weigh(group - 1)
        rotate(groups - 1)
        line_up(groups - 1)
        score(groups - 1)
        weigh(groups - 1)

    for_row_bound(total, rows, run)


def attend(plan, near, far, w_qkv, part, senders):
    rows = far.shape[0]
    block = (QUERY_PER_KEY + 2) * HEAD_SIZE
    depth, columns = w_qkv.shape
    groups = columns // block
    out_columns = groups * QUERY_PER_KEY * HEAD_SIZE
    padded = rows + WINDOW
    pair = 2 * HEAD_SIZE
    tiles = rows // TILE
    cos, sine = rotary_tables(rows)
    return pl.pallas_call(
        attend_body,
        in_specs=[SCALARS] + [WHOLE] * 6,
        out_specs=WHOLE,
        scratch_shapes=[
            pltpu.VMEM((rows, HEAD_SIZE), jnp.float32),
            pltpu.VMEM((pair, pair), jnp.bfloat16),
            pltpu.VMEM((tiles, TILE, WINDOW), jnp.bfloat16),
            pltpu.VMEM((groups, rows, block), jnp.float32),
            pltpu.VMEM((groups, padded, block), jnp.bfloat16),
            pltpu.VMEM((groups, rows, 2 * pair), jnp.bfloat16),
            pltpu.VMEM((groups, tiles, pair, pair), jnp.bfloat16),
            pltpu.VMEM((groups, tiles, pair, pair), jnp.bfloat16),
            pltpu.VMEM((groups, tiles, pair, pair), jnp.float32),
        ],
        out_shape=jax.ShapeDtypeStruct((senders, IMG_MAX, out_columns), jnp.bfloat16),
        compiler_params=limit(20),
        cost_estimate=pl.CostEstimate(
            flops=rows * depth * columns, bytes_accessed=depth * columns, transcendentals=0
        ),
        name="attend",
    )(plan, near, far, w_qkv, part, cos, sine)


def place_body(counts_ref, shift_ref, box_ref, out_hbm, placed, sems):
    senders = box_ref.shape[0]
    per_tile = counts_ref.shape[0]
    tiles = shift_ref.shape[0] // per_tile
    me = lax.axis_index("dp")
    lane = lax.broadcasted_iota(jnp.int32, (TILE, TILE), 1)
    row = lax.broadcasted_iota(jnp.int32, (TILE, TILE), 0)
    inside = jnp.bitwise_and(lane, IMG_MAX - 1)
    image = lane // IMG_MAX
    copies = []
    for tile in range(tiles):
        goal = jnp.full((TILE, TILE), -1, jnp.int32)
        offset = jnp.int32(0)
        blocks = []
        for j in range(per_tile):
            count = counts_ref[j, me * tiles + tile]
            goal = jnp.where((image == j) & (inside < count), inside + offset, goal)
            offset = offset + count
            source = lax.rem(me + shift_ref[tile * per_tile + j], senders)
            blocks.append(box_ref[source])
        at = pl.ds(tile * TILE, TILE)
        placed[at, :] = jnp.dot(
            jnp.where(row == goal, 1.0, 0.0).astype(jnp.bfloat16),
            jnp.concatenate(blocks, axis=0),
            preferred_element_type=jnp.float32,
        ).astype(jnp.bfloat16)
        copy = pltpu.make_async_copy(placed.at[at], out_hbm.at[at], sems.at[tile])
        copy.start()
        copies.append(copy)
    for copy in copies:
        copy.wait()


def place_rows(counts, shift, box):
    senders, depth, columns = box.shape
    rows = shift.shape[0] * depth
    return pl.pallas_call(
        place_body,
        in_specs=[SCALARS] * 2 + [WHOLE],
        out_specs=FAR_MEMORY,
        out_shape=jax.ShapeDtypeStruct((rows, columns), jnp.bfloat16),
        scratch_shapes=[
            pltpu.VMEM((rows, columns), jnp.bfloat16),
            pltpu.SemaphoreType.DMA((rows // TILE,)),
        ],
        compiler_params=limit(8),
        name="place_rows",
    )(counts, shift, box)


def local(
    patches, ln_gain, ln_bias, w_proj, proj_bias, rms_gain, w_qkv, image_counts, source_shift
):
    senders = lax.axis_size("dp")
    counts = image_counts.T
    other = lax.ppermute(patches, "mp", SWAP)
    pin = lambda x: pltpu.with_memory_space_constraint(x, pltpu.HBM)
    own = norm_own(pin(patches), pin(ln_gain), pin(ln_bias))
    normed, plan = norm_other(counts, source_shift, own, other, ln_gain, ln_bias)
    near = project(plan, normed, w_proj, proj_bias, rms_gain)
    far = lax.ppermute(near, "mp", SWAP)
    part = first_half(plan, near, w_qkv)
    outbox = attend(plan, near, far, w_qkv, part, senders)
    in_box = lax.all_to_all(outbox, "dp", split_axis=0, concat_axis=0, tiled=True)
    return place_rows(counts, source_shift, in_box)


def solution(mesh):
    in_specs = (
        P(("dp", "mp"), None),
        P(),
        P(),
        P(None, "mp"),
        P("mp"),
        P(),
        P(None, "mp"),
        P(),
        P(),
    )
    out_specs = P("dp", "mp")
    return jax.shard_map(local, mesh=mesh, in_specs=in_specs, out_specs=out_specs, check_vma=False)
```

time: 68.9 us -> 67.2 us (0.975)
  Pallas kernels: 26 us -> 22.6 us
  waiting for transfers between devices: 0.17 us -> 2.1 us
    pallas_call x4, Pallas kernels: 20.6 us -> 18.1 us  [the longest x1 6.18 us: project(): pl.pallas_call(project_body, in_specs=[SCALARS] + [WHOLE] * 4, out_specs=...]
    ppermute x1, waiting for transfers between devices: 0.01 us -> 1.05 us  [local(): far = lax.ppermute(near, 'mp', SWAP)]
    ppermute x1, waiting for transfers between devices: 0.16 us -> 1.05 us  [local(): other = lax.ppermute(patches, 'mp', SWAP)]
    pallas_call x1, Pallas kernels: 3.49 us -> 2.61 us  [norm_own(): pl.pallas_call(norm_own_body, in_specs=[FAR_MEMORY] * 3, out_specs=WHOLE,...]
  transfers between devices with their start and end apart: 2 -> 2, of which waited for: 1 -> 2; matrix products, arithmetic and copies ran while one was open for 0% -> 0% of each run, Pallas kernels for 11% -> 9%
where the time goes in v4:
time: 67.2 us; the launch traced here: 67.1 us
  blocking collectives  41.7 us (62%)
  Pallas kernels  22.6 us (34%)
  waiting for transfers between devices  2.1 us (3%)
    all_to_all x1, blocking collectives, local(): lax.all_to_all(outbox, 'dp', split_axis=0, concat_axis=0, tiled=True)  41.7 us
    pallas_call x1, Pallas kernels, project(): pl.pallas_call(project_body, in_specs=[SCALARS] + [WHOLE] * 4, out_specs=...  6.18 us
    pallas_call x1, Pallas kernels, attend(): pl.pallas_call(attend_body, in_specs=[SCALARS] + [WHOLE] * 6, out_specs=W...  5.88 us
    pallas_call x1, Pallas kernels, first_half(): pl.pallas_call(first_half_body, in_specs=[SCALARS] + [WHOLE] * 2, out_spe...  3.15 us
    pallas_call x1, Pallas kernels, norm_other(): pl.pallas_call(norm_other_body, in_specs=[SCALARS] * 2 + [WHOLE] * 4, out...  2.87 us
    pallas_call x1, Pallas kernels, norm_own(): pl.pallas_call(norm_own_body, in_specs=[FAR_MEMORY] * 3, out_specs=WHOLE,...  2.61 us
    pallas_call x1, Pallas kernels, place_rows(): pl.pallas_call(place_body, in_specs=[SCALARS] * 2 + [WHOLE], out_specs=FA...  1.91 us
  transfers between devices with their start and end apart: 2, of which 2 were waited for; matrix products, arithmetic and copies ran while one was open for 0% of the time, Pallas kernels for 9%

profile of v4, /device:TPU:0, one launch (start us, length us, event | category | flops | bytes accessed | tf_op | source)
XLA Modules:
  0.0 67.1 jit_solution(6166258931806960618)
XLA Ops:
  0.0 0.0 copy-start.4
  0.0 0.0 copy-start.3
  0.0 0.0 copy-start.5
  0.0 0.0 copy-start.2
  0.0 0.1 collective-permute-start
  0.1 0.0 copy-start.6
  0.1 2.6 %norm_own.1.own_ref = bf16[256,3200]{1,0:T(8,128)(2,1)S(1)} custom-call(bf16[256,3200]{1,0:T(8,128)(2,1)} %rows_hbm.1, bf16[3200]{0:T(1024)(128)(2,1)} %gain_ref.1, bf16[3200]{0:T(1024)(128)(2,1)} %bias_ref.1), custom_call_target="tpu_custom_call" | custom-call | flops 8000000000 | bytes 3276800 | tf_op jit(solution)/shard_map/norm_own/pallas_call | solution.py:120
  2.7 0.0 copy-start.7
  2.7 0.0 copy-start.8
  2.7 1.0 %collective-permute-done.other_ref = bf16[256,3200]{1,0:T(8,128)(2,1)S(1)} collective-permute-done((bf16[256,3200]{1,0:T(8,128)(2,1)}, bf16[256,3200]{1,0:T(8,128)(2,1)S(1)}, u32[]{:S(2)}, u32[]{:S(2)}) %collective-permute-start) | collective-permute-done | bytes 1638432 | tf_op jit(solution)/shard_map/ppermute | solution.py:530
  3.8 0.0 copy-done.4
  3.8 0.0 copy-done.3
  3.8 0.0 copy-done.5
  3.8 0.0 copy-done.2
  3.8 0.0 slice-start
  3.8 2.9 %norm_other.1 = (bf16[512,3200]{1,0:T(8,128)(2,1)S(1)}, s32[65]{0:T(128)S(1)}) custom-call(s32[8,256]{1,0:T(8,128)S(1)} %bitcast.3, s32[32]{0:T(128)S(1)} %copy-done.5, bf16[256,3200]{1,0:T(8,128)(2,1)S(1)} %norm_own.1.own_ref, bf16[256,3200]{1,0:T(8,128)(2,1)S(1)} %collective-permute-done.other_ref, bf16[3200]{0:T(1024)(128)(2,1)S(1)} %copy-done.3, ...), custom_call_target="tpu_custom_call" | custom-call | flops 8192000 | bytes 3276800 | tf_op jit(solution)/shard_map/norm_other/pallas_call | solution.py:159
  6.7 0.0 copy-done.6
  6.7 0.0 copy-done.7
  6.7 0.0 copy-done.8
  6.7 0.0 slice-start.1
  6.8 0.0 slice-start.2
  6.8 6.2 %project.1.gained_ref.near_ref = bf16[512,2176]{1,0:T(8,128)(2,1)S(1)} custom-call(s32[65]{0:T(128)S(1)} %get-tuple-element.7.plan_ref, bf16[512,3200]{1,0:T(8,128)(2,1)S(1)} %get-tuple-element.8.normed_ref, bf16[3200,2048]{1,0:T(8,128)(2,1)S(1)} %copy-done.6, bf16[2048]{0:T(1024)(128)(2,1)S(1)} %copy-done.8, bf16[4096]{0:T(1024)(128)(2,1)S(1)} %copy-done.7), custom_call_target="tpu_custom_call" | custom-call | flops 6710886400 | bytes 13107200 | tf_op jit(solution)/shard_map/project/pallas_call | solution.py:240
  13.0 0.0 copy-start
  13.0 0.0 copy-start.1
  13.0 0.2 collective-permute-start.1
  13.2 0.0 slice-done
  13.2 0.0 slice-done.1
  13.2 0.0 slice-done.2
  13.2 3.2 %first_half.1.part_ref = f32[512,1536]{1,0:T(8,128)S(1)} custom-call(s32[65]{0:T(128)S(1)} %get-tuple-element.7.plan_ref, bf16[512,2176]{1,0:T(8,128)(2,1)S(1)} %project.1.gained_ref.near_ref, bf16[4096,1536]{1,0:T(8,128)(2,1)S(1)} %bitcast.2), custom_call_target="tpu_custom_call" | custom-call | flops 3221225472 | bytes 9437184 | tf_op jit(solution)/shard_map/first_half/pallas_call | solution.py:286
  16.4 1.1 %collective-permute-done.1.far_ref = bf16[512,2176]{1,0:T(8,128)(2,1)S(1)} collective-permute-done((bf16[512,2176]{1,0:T(8,128)(2,1)S(1)}, bf16[512,2176]{1,0:T(8,128)(2,1)S(1)}, u32[]{:S(2)}, u32[]{:S(2)}) %collective-permute-start.1) | collective-permute-done | bytes 2228256 | tf_op jit(solution)/shard_map/ppermute | solution.py:535
  17.4 0.0 copy-done
  17.4 0.0 copy-done.1
  17.4 5.9 %attend.1 = bf16[64,16,1024]{2,1,0:T(8,128)(2,1)S(1)} custom-call(s32[65]{0:T(128)S(1)} %get-tuple-element.7.plan_ref, bf16[512,2176]{1,0:T(8,128)(2,1)S(1)} %project.1.gained_ref.near_ref, bf16[512,2176]{1,0:T(8,128)(2,1)S(1)} %collective-permute-done.1.far_ref, bf16[4096,1536]{1,0:T(8,128)(2,1)S(1)} %bitcast.2, f32[512,1536]{1,0:T(8,128)S(1)} %first_half.1.part_ref, ...), custom_call_target="tpu_custom_call" | custom-call | flops 3221225472 | bytes 6291456 | tf_op jit(solution)/shard_map/attend/pallas_call | solution.py:451
  23.3 41.7 %all_to_all.5.box_ref = bf16[64,16,1024]{2,1,0:T(8,128)(2,1)S(1)} all-to-all(bf16[64,16,1024]{2,1,0:T(8,128)(2,1)S(1)} %attend.1), channel_id=1, replica_groups=mesh['dp'=64,'mp'=2] {'dp'}, dimensions={0} | all-to-all | bytes 4194304 | tf_op jit(solution)/shard_map/all_to_all | solution.py:538
  65.0 1.9 %place_rows.1 = bf16[512,1024]{1,0:T(8,128)(2,1)} custom-call(s32[8,256]{1,0:T(8,128)S(1)} %bitcast.4, s32[32]{0:T(128)S(1)} %copy-done.5, bf16[64,16,1024]{2,1,0:T(8,128)(2,1)S(1)} %all_to_all.5.box_ref), custom_call_target="tpu_custom_call" | custom-call | tf_op jit(solution)/shard_map/place_rows/pallas_call | solution.py:511
  (1 shorter events, 0.0 us)
Async XLA Ops:
  0.0 3.8 %copy-start.4 = (bf16[3200]{0:T(1024)(128)(2,1)S(1)}, bf16[3200]{0:T(1024)(128)(2,1)}, u32[]{:S(2)}) copy-start(bf16[3200]{0:T(1024)(128)(2,1)} %bias_ref.1) | copy-start | bytes 19204
  0.0 3.8 %copy-start.3 = (bf16[3200]{0:T(1024)(128)(2,1)S(1)}, bf16[3200]{0:T(1024)(128)(2,1)}, u32[]{:S(2)}) copy-start(bf16[3200]{0:T(1024)(128)(2,1)} %gain_ref.1) | copy-start | bytes 19204
  0.0 3.8 %copy-start.5 = (s32[32]{0:T(128)S(1)}, s32[32]{0:T(128)}, u32[]{:S(2)}) copy-start(s32[32]{0:T(128)} %shift_ref.3) | copy-start | bytes 388
  0.0 3.8 %copy-start.2 = (s32[256,8]{0,1:T(8,128)S(1)}, s32[256,8]{0,1:T(8,128)}, u32[]{:S(2)}) copy-start(s32[256,8]{0,1:T(8,128)} %param.18) | copy-start | bytes 24580
  0.0 3.8 %collective-permute-start = (bf16[256,3200]{1,0:T(8,128)(2,1)}, bf16[256,3200]{1,0:T(8,128)(2,1)S(1)}, u32[]{:S(2)}, u32[]{:S(2)}) collective-permute-start(bf16[256,3200]{1,0:T(8,128)(2,1)} %rows_hbm.1), channel_id=1, source_target_pairs={{0,1},{1,0},{2,3},{3,2},{4,5},{5,4},{6,7},{7,6},{8,9},{9,8},{10,11... | collective-permute-start | bytes 4915208 | tf_op jit(solution)/shard_map/ppermute | solution.py:530
  0.1 6.6 %copy-start.6 = (bf16[3200,2048]{1,0:T(8,128)(2,1)S(1)}, bf16[3200,2048]{1,0:T(8,128)(2,1)}, u32[]{:S(2)}) copy-start(bf16[3200,2048]{1,0:T(8,128)(2,1)} %w_ref.3) | copy-start | bytes 39321604
  2.7 4.0 %copy-start.7 = (bf16[4096]{0:T(1024)(128)(2,1)S(1)}, bf16[4096]{0:T(1024)(128)(2,1)}, u32[]{:S(2)}) copy-start(bf16[4096]{0:T(1024)(128)(2,1)} %rms_ref.1) | copy-start | bytes 24580
  2.7 4.0 %copy-start.8 = (bf16[2048]{0:T(1024)(128)(2,1)S(1)}, bf16[2048]{0:T(1024)(128)(2,1)}, u32[]{:S(2)}) copy-start(bf16[2048]{0:T(1024)(128)(2,1)} %add_ref.1) | copy-start | bytes 12292
  3.8 9.4 %slice-start = ((s8[12582912]{0:T(1024)(128)(4,1)}), s8[4194304]{0:T(1024)(128)(4,1)S(1)}, s32[]{:S(2)}) async-start(s8[12582912]{0:T(1024)(128)(4,1)} %bitcast.1), calls=%async_computation.1 | async-start | bytes 8388608
  6.7 6.4 %slice-start.1 = ((s8[12582912]{0:T(1024)(128)(4,1)}), s8[4194304]{0:T(1024)(128)(4,1)S(1)}, s32[]{:S(2)}) async-start(s8[12582912]{0:T(1024)(128)(4,1)} %bitcast.1), calls=%async_computation.2 | async-start | bytes 8388608
  6.8 6.4 %slice-start.2 = ((s8[12582912]{0:T(1024)(128)(4,1)}), s8[4194304]{0:T(1024)(128)(4,1)S(1)}, s32[]{:S(2)}) async-start(s8[12582912]{0:T(1024)(128)(4,1)} %bitcast.1), calls=%async_computation.3 | async-start | bytes 8388608
  13.0 4.5 %copy-start = (f32[512,128]{1,0:T(8,128)S(1)}, f32[512,128]{1,0:T(8,128)}, u32[]{:S(2)}) copy-start(f32[512,128]{1,0:T(8,128)} %constant.5.clone.sine_ref) | copy-start | bytes 786436
  13.0 4.4 %copy-start.1 = (f32[512,128]{1,0:T(8,128)S(1)}, f32[512,128]{1,0:T(8,128)}, u32[]{:S(2)}) copy-start(f32[512,128]{1,0:T(8,128)} %constant.4.clone.cos_ref) | copy-start | bytes 786436
  13.0 4.4 %collective-permute-start.1 = (bf16[512,2176]{1,0:T(8,128)(2,1)S(1)}, bf16[512,2176]{1,0:T(8,128)(2,1)S(1)}, u32[]{:S(2)}, u32[]{:S(2)}) collective-permute-start(bf16[512,2176]{1,0:T(8,128)(2,1)S(1)} %project.1.gained_ref.near_ref), channel_id=1, source_target_pairs={{0,1},{1,0},{2,3},{3,2},{4,5},{5,4},{6,7},{7,6},{8,9},{9,8},{10,11... | collective-permute-start | bytes 6684680 | tf_op jit(solution)/shard_map/ppermute | solution.py:535

commit v5 on v4

--- a/solution.py
+++ b/solution.py
@@ -44,19 +44,38 @@
     return jnp.asarray(cos.astype(np.float32)), jnp.asarray(sine.astype(np.float32))
 
 
-def write_plan(counts_ref, shift_ref, plan_ref):
+def plan_body(counts_ref, shift_ref, after_ref, plan_ref):
+    del after_ref
     images = shift_ref.shape[0]
     tile_images = counts_ref.shape[0]
     tiles = images // tile_images
     senders = counts_ref.shape[1] // tiles
     me = lax.axis_index("dp")
+    shifts = [shift_ref[k] for k in range(images)]
+    targets = [lax.rem(me - shift + senders, senders) for shift in shifts]
+    places = [(k % tile_images, k // tile_images) for k in range(images)]
+    sent = [counts_ref[row, to * tiles + at] for to, (row, at) in zip(targets, places)]
+    mine = [counts_ref[row, me * tiles + at] for row, at in places]
     start = jnp.int32(0)
     for k in range(images):
         plan_ref[k] = start
-        target = lax.rem(me - shift_ref[k] + senders, senders)
-        plan_ref[images + 1 + k] = target
-        start = start + counts_ref[k % tile_images, target * tiles + k // tile_images]
+        plan_ref[images + 1 + k] = targets[k]
+        plan_ref[2 * images + 1 + k] = mine[k]
+        plan_ref[3 * images + 1 + k] = lax.rem(me + shifts[k], senders)
+        start = start + sent[k]
     plan_ref[images] = start
+
+
+def make_plan(counts, shift, after):
+    return pl.pallas_call(
+        plan_body,
+        in_specs=[SCALARS] * 2 + [pl.BlockSpec(memory_space=pl.ANY)],
+        out_specs=SCALARS,
+        out_shape=jax.ShapeDtypeStruct((4 * shift.shape[0] + 1,), jnp.int32),
+        compiler_params=limit(1),
+        cost_estimate=pl.CostEstimate(flops=10_000, bytes_accessed=10_000, transcendentals=0),
+        name="make_plan",
+    )(counts, shift, after)
 
 
 def for_row_bound(total, most, run):
@@ -138,11 +157,7 @@
     )(rows, gain, bias)
 
 
-def norm_other_body(
-    counts_ref, shift_ref, own_ref, other_ref, gain_ref, bias_ref, out_ref, plan_ref,
-    gain_row, bias_row,
-):
-    write_plan(counts_ref, shift_ref, plan_ref)
+def norm_other_body(own_ref, other_ref, gain_ref, bias_ref, out_ref, gain_row, bias_row):
     half, width = own_ref.shape
     core = lax.axis_index("mp")
     out_ref[pl.ds(pl.multiple_of(core * half, half), half), :] = own_ref[...]
@@ -153,24 +168,20 @@
     )
 
 
-def norm_other(counts, shift, own, other, gain, bias):
+def norm_other(own, other, gain, bias):
     half, width = own.shape
-    images = shift.shape[0]
     return pl.pallas_call(
         norm_other_body,
-        in_specs=[SCALARS] * 2 + [WHOLE] * 4,
-        out_specs=[WHOLE, SCALARS],
-        out_shape=[
-            jax.ShapeDtypeStruct((2 * half, width), jnp.bfloat16),
-            jax.ShapeDtypeStruct((2 * images + 1,), jnp.int32),
-        ],
+        in_specs=[WHOLE] * 4,
+        out_specs=WHOLE,
+        out_shape=jax.ShapeDtypeStruct((2 * half, width), jnp.bfloat16),
         scratch_shapes=[pltpu.VMEM((1, width), jnp.float32)] * 2,
         compiler_params=limit(6),
         cost_estimate=pl.CostEstimate(
             flops=10 * half * width, bytes_accessed=4 * half * width, transcendentals=0
         ),
         name="norm_other",
-    )(counts, shift, own, other, gain, bias)
+    )(own, other, gain, bias)
 
 
 def project_body(
@@ -179,7 +190,7 @@
 ):
     rows = normed_ref.shape[0]
     columns = w_ref.shape[1]
-    total = plan_ref[plan_ref.shape[0] // 2]
+    total = plan_ref[plan_ref.shape[0] // 4]
     mine = pl.multiple_of(lax.axis_index("mp") * columns, columns)
     add_row[...] = add_ref[...].reshape(1, columns).astype(jnp.float32)
     rms_row[...] = rms_ref[...].reshape(1, 2 * columns).astype(jnp.float32)
@@ -263,7 +274,7 @@
     rows = gained_ref.shape[0]
     depth = w_ref.shape[0] // 2
     mine = pl.multiple_of(lax.axis_index("mp") * depth, depth)
-    total = plan_ref[plan_ref.shape[0] // 2]
+    total = plan_ref[plan_ref.shape[0] // 4]
 
     def run(bound):
         def block(j, carry):
@@ -305,7 +316,7 @@
     groups, padded, width = turned_rows.shape
     rows = far_ref.shape[0]
     depth = w_ref.shape[0] // 2
-    images = plan_ref.shape[0] // 2
+    images = plan_ref.shape[0] // 4
     per_tile = TILE // IMG_MAX
     tiles = rows // TILE
     pair = 2 * HEAD_SIZE
@@ -424,16 +435,15 @@
         prepare()
         turned_rows[:, bound:, :] = jnp.zeros((groups, padded - bound, width), jnp.bfloat16)
         for group in range(1, groups):
-            product(group, 0, 512)
+            product(group, 0, width)
             rotate(group - 1)
             line_up(group - 1)
             score(group - 1)
-            product(group, 512, width)
-            weigh(group - 1)
         rotate(groups - 1)
         line_up(groups - 1)
         score(groups - 1)
-        weigh(groups - 1)
+        for group in range(groups):
+            weigh(group)
 
     for_row_bound(total, rows, run)
 
@@ -472,11 +482,10 @@
     )(plan, near, far, w_qkv, part, cos, sine)
 
 
-def place_body(counts_ref, shift_ref, box_ref, out_hbm, placed, sems):
-    senders = box_ref.shape[0]
-    per_tile = counts_ref.shape[0]
-    tiles = shift_ref.shape[0] // per_tile
-    me = lax.axis_index("dp")
+def place_body(plan_ref, box_ref, out_hbm, placed, sems):
+    images = plan_ref.shape[0] // 4
+    per_tile = TILE // IMG_MAX
+    tiles = images // per_tile
     lane = lax.broadcasted_iota(jnp.int32, (TILE, TILE), 1)
     row = lax.broadcasted_iota(jnp.int32, (TILE, TILE), 0)
     inside = jnp.bitwise_and(lane, IMG_MAX - 1)
@@ -487,11 +496,10 @@
         offset = jnp.int32(0)
         blocks = []
         for j in range(per_tile):
-            count = counts_ref[j, me * tiles + tile]
+            count = plan_ref[2 * images + 1 + tile * per_tile + j]
             goal = jnp.where((image == j) & (inside < count), inside + offset, goal)
             offset = offset + count
-            source = lax.rem(me + shift_ref[tile * per_tile + j], senders)
-            blocks.append(box_ref[source])
+            blocks.append(box_ref[plan_ref[3 * images + 1 + tile * per_tile + j]])
         at = pl.ds(tile * TILE, TILE)
         placed[at, :] = jnp.dot(
             jnp.where(row == goal, 1.0, 0.0).astype(jnp.bfloat16),
@@ -505,12 +513,12 @@
         copy.wait()
 
 
-def place_rows(counts, shift, box):
-    senders, depth, columns = box.shape
-    rows = shift.shape[0] * depth
+def place_rows(plan, box):
+    depth, columns = box.shape[1:]
+    rows = plan.shape[0] // 4 * depth
     return pl.pallas_call(
         place_body,
-        in_specs=[SCALARS] * 2 + [WHOLE],
+        in_specs=[SCALARS, WHOLE],
         out_specs=FAR_MEMORY,
         out_shape=jax.ShapeDtypeStruct((rows, columns), jnp.bfloat16),
         scratch_shapes=[
@@ -519,7 +527,7 @@
         ],
         compiler_params=limit(8),
         name="place_rows",
-    )(counts, shift, box)
+    )(plan, box)
 
 
 def local(
@@ -530,13 +538,14 @@
     other = lax.ppermute(patches, "mp", SWAP)
     pin = lambda x: pltpu.with_memory_space_constraint(x, pltpu.HBM)
     own = norm_own(pin(patches), pin(ln_gain), pin(ln_bias))
-    normed, plan = norm_other(counts, source_shift, own, other, ln_gain, ln_bias)
+    plan = make_plan(counts, source_shift, own)
+    normed = norm_other(own, other, ln_gain, ln_bias)
     near = project(plan, normed, w_proj, proj_bias, rms_gain)
     far = lax.ppermute(near, "mp", SWAP)
     part = first_half(plan, near, w_qkv)
     outbox = attend(plan, near, far, w_qkv, part, senders)
     in_box = lax.all_to_all(outbox, "dp", split_axis=0, concat_axis=0, tiled=True)
-    return place_rows(counts, source_shift, in_box)
+    return place_rows(plan, in_box)
 
 
 def solution(mesh):

time: 67.2 us -> 66.6 us (level)
  waiting for transfers between devices: 2.1 us -> 0.8 us
    ppermute x1, waiting for transfers between devices: 1.05 us -> 0.01 us  [local(): other = lax.ppermute(patches, 'mp', SWAP)]
    pallas_call x2 -> x3, Pallas kernels: 4.78 us -> 5.16 us  [the longest x1 1.77 us: norm_other(): pl.pallas_call(norm_other_body, in_specs=[WHOLE] * 4, out_specs=WHOLE, ou...]
  transfers between devices with their start and end apart: 2 -> 2, of which waited for: 2 -> 1; matrix products, arithmetic and copies ran while one was open for 0% -> 0% of each run, Pallas kernels for 9% -> 11%
where the time goes in v5:
time: 66.6 us; the launch traced here: 66.5 us
  blocking collectives  42 us (63%)
  Pallas kernels  22.6 us (34%)
  waiting for transfers between devices  0.8 us (1%)
    all_to_all x1, blocking collectives, local(): lax.all_to_all(outbox, 'dp', split_axis=0, concat_axis=0, tiled=True)  42 us
    pallas_call x1, Pallas kernels, project(): pl.pallas_call(project_body, in_specs=[SCALARS] + [WHOLE] * 4, out_specs=...  6.24 us
    pallas_call x1, Pallas kernels, attend(): pl.pallas_call(attend_body, in_specs=[SCALARS] + [WHOLE] * 6, out_specs=W...  5.4 us
    pallas_call x1, Pallas kernels, first_half(): pl.pallas_call(first_half_body, in_specs=[SCALARS] + [WHOLE] * 2, out_spe...  3.16 us
    pallas_call x1, Pallas kernels, norm_own(): pl.pallas_call(norm_own_body, in_specs=[FAR_MEMORY] * 3, out_specs=WHOLE,...  2.61 us
    pallas_call x1, Pallas kernels, norm_other(): pl.pallas_call(norm_other_body, in_specs=[WHOLE] * 4, out_specs=WHOLE, ou...  1.77 us
    pallas_call x1, Pallas kernels, place_rows(): pl.pallas_call(place_body, in_specs=[SCALARS, WHOLE], out_specs=FAR_MEMOR...  1.77 us
    pallas_call x1, Pallas kernels, make_plan(): pl.pallas_call(plan_body, in_specs=[SCALARS] * 2 + [pl.BlockSpec(memory_s...  1.62 us
  transfers between devices with their start and end apart: 2, of which 1 were waited for; matrix products, arithmetic and copies ran while one was open for 0% of the time, Pallas kernels for 11%

profile of v5, /device:TPU:0, one launch (start us, length us, event | category | flops | bytes accessed | tf_op | source)
XLA Modules:
  0.0 66.5 jit_solution(16052749470456778061)
XLA Ops:
  0.0 0.0 copy-start.4
  0.0 0.0 copy-start.3
  0.0 0.0 copy-start.5
  0.0 0.0 copy-start.2
  0.0 0.1 collective-permute-start
  0.1 0.0 copy-start.6
  0.1 2.6 %norm_own.1.after_ref.own_ref = bf16[256,3200]{1,0:T(8,128)(2,1)S(1)} custom-call(bf16[256,3200]{1,0:T(8,128)(2,1)} %rows_hbm.1, bf16[3200]{0:T(1024)(128)(2,1)} %gain_ref.1, bf16[3200]{0:T(1024)(128)(2,1)} %bias_ref.1), custom_call_target="tpu_custom_call" | custom-call | flops 8000000000 | bytes 3276800 | tf_op jit(solution)/shard_map/norm_own/pallas_call | solution.py:139
  2.7 0.0 copy-done.5
  2.7 0.0 copy-done.2
  2.7 1.6 %make_plan.1.plan_ref = s32[129]{0:T(256)S(1)} custom-call(s32[8,256]{1,0:T(8,128)S(1)} %bitcast.3, s32[32]{0:T(128)S(1)} %copy-done.5, bf16[256,3200]{1,0:T(8,128)(2,1)S(1)} %norm_own.1.after_ref.own_ref), custom_call_target="tpu_custom_call" | custom-call | flops 10000 | bytes 10000 | tf_op jit(solution)/shard_map/make_plan/pallas_call | solution.py:70
  4.4 0.0 copy-start.7
  4.4 0.0 copy-start.8
  4.4 0.0 collective-permute-done.other_ref
  4.4 0.0 copy-done.4
  4.4 0.0 copy-done.3
  4.4 0.0 slice-start
  4.4 1.8 %norm_other.1.normed_ref = bf16[512,3200]{1,0:T(8,128)(2,1)S(1)} custom-call(bf16[256,3200]{1,0:T(8,128)(2,1)S(1)} %norm_own.1.after_ref.own_ref, bf16[256,3200]{1,0:T(8,128)(2,1)S(1)} %collective-permute-done.other_ref, bf16[3200]{0:T(1024)(128)(2,1)S(1)} %copy-done.3, bf16[3200]{0:T(1024)(128)(2,1)S(1)} %copy-done.4), custom_call_target="tpu_custom_call" | custom-call | flops 8192000 | bytes 3276800 | tf_op jit(solution)/shard_map/norm_other/pallas_call | solution.py:173
  6.2 0.0 copy-done.6
  6.2 0.0 copy-done.7
  6.2 0.0 copy-done.8
  6.2 0.0 slice-start.1
  6.3 0.0 slice-start.2
  6.3 6.2 %project.1.gained_ref.near_ref = bf16[512,2176]{1,0:T(8,128)(2,1)S(1)} custom-call(s32[129]{0:T(256)S(1)} %make_plan.1.plan_ref, bf16[512,3200]{1,0:T(8,128)(2,1)S(1)} %norm_other.1.normed_ref, bf16[3200,2048]{1,0:T(8,128)(2,1)S(1)} %copy-done.6, bf16[2048]{0:T(1024)(128)(2,1)S(1)} %copy-done.8, bf16[4096]{0:T(1024)(128)(2,1)S(1)} %copy-done.7), custom_call_target="tpu_custom_call" | custom-call | flops 6710886400 | bytes 13107200 | tf_op jit(solution)/shard_map/project/pallas_call | solution.py:251
  12.5 0.0 copy-start
  12.5 0.0 copy-start.1
  12.5 0.6 collective-permute-start.1
  13.1 0.0 slice-done
  13.1 0.0 slice-done.1
  13.1 0.0 slice-done.2
  13.1 3.2 %first_half.1.part_ref = f32[512,1536]{1,0:T(8,128)S(1)} custom-call(s32[129]{0:T(256)S(1)} %make_plan.1.plan_ref, bf16[512,2176]{1,0:T(8,128)(2,1)S(1)} %project.1.gained_ref.near_ref, bf16[4096,1536]{1,0:T(8,128)(2,1)S(1)} %bitcast.2), custom_call_target="tpu_custom_call" | custom-call | flops 3221225472 | bytes 9437184 | tf_op jit(solution)/shard_map/first_half/pallas_call | solution.py:297
  16.3 0.8 %collective-permute-done.1.far_ref = bf16[512,2176]{1,0:T(8,128)(2,1)S(1)} collective-permute-done((bf16[512,2176]{1,0:T(8,128)(2,1)S(1)}, bf16[512,2176]{1,0:T(8,128)(2,1)S(1)}, u32[]{:S(2)}, u32[]{:S(2)}) %collective-permute-start.1) | collective-permute-done | bytes 2228256 | tf_op jit(solution)/shard_map/ppermute | solution.py:544
  17.1 0.0 copy-done
  17.1 0.0 copy-done.1
  17.1 5.4 %attend.1 = bf16[64,16,1024]{2,1,0:T(8,128)(2,1)S(1)} custom-call(s32[129]{0:T(256)S(1)} %make_plan.1.plan_ref, bf16[512,2176]{1,0:T(8,128)(2,1)S(1)} %project.1.gained_ref.near_ref, bf16[512,2176]{1,0:T(8,128)(2,1)S(1)} %collective-permute-done.1.far_ref, bf16[4096,1536]{1,0:T(8,128)(2,1)S(1)} %bitcast.2, f32[512,1536]{1,0:T(8,128)S(1)} %first_half.1.part_ref, ...), custom_call_target="tpu_custom_call" | custom-call | flops 3221225472 | bytes 6291456 | tf_op jit(solution)/shard_map/attend/pallas_call | solution.py:461
  22.5 42.0 %all_to_all.5.box_ref = bf16[64,16,1024]{2,1,0:T(8,128)(2,1)S(1)} all-to-all(bf16[64,16,1024]{2,1,0:T(8,128)(2,1)S(1)} %attend.1), channel_id=1, replica_groups=mesh['dp'=64,'mp'=2] {'dp'}, dimensions={0} | all-to-all | bytes 4194304 | tf_op jit(solution)/shard_map/all_to_all | solution.py:547
  64.5 1.8 %place_rows.1 = bf16[512,1024]{1,0:T(8,128)(2,1)} custom-call(s32[129]{0:T(256)S(1)} %make_plan.1.plan_ref, bf16[64,16,1024]{2,1,0:T(8,128)(2,1)S(1)} %all_to_all.5.box_ref), custom_call_target="tpu_custom_call" | custom-call | tf_op jit(solution)/shard_map/place_rows/pallas_call | solution.py:519
  (1 shorter events, 0.0 us)
Async XLA Ops:
  0.0 4.4 %copy-start.4 = (bf16[3200]{0:T(1024)(128)(2,1)S(1)}, bf16[3200]{0:T(1024)(128)(2,1)}, u32[]{:S(2)}) copy-start(bf16[3200]{0:T(1024)(128)(2,1)} %bias_ref.1) | copy-start | bytes 19204
  0.0 4.4 %copy-start.3 = (bf16[3200]{0:T(1024)(128)(2,1)S(1)}, bf16[3200]{0:T(1024)(128)(2,1)}, u32[]{:S(2)}) copy-start(bf16[3200]{0:T(1024)(128)(2,1)} %gain_ref.1) | copy-start | bytes 19204
  0.0 2.7 %copy-start.5 = (s32[32]{0:T(128)S(1)}, s32[32]{0:T(128)}, u32[]{:S(2)}) copy-start(s32[32]{0:T(128)} %shift_ref.1) | copy-start | bytes 388
  0.0 2.7 %copy-start.2 = (s32[256,8]{0,1:T(8,128)S(1)}, s32[256,8]{0,1:T(8,128)}, u32[]{:S(2)}) copy-start(s32[256,8]{0,1:T(8,128)} %param.18) | copy-start | bytes 24580
  0.0 4.4 %collective-permute-start = (bf16[256,3200]{1,0:T(8,128)(2,1)}, bf16[256,3200]{1,0:T(8,128)(2,1)S(1)}, u32[]{:S(2)}, u32[]{:S(2)}) collective-permute-start(bf16[256,3200]{1,0:T(8,128)(2,1)} %rows_hbm.1), channel_id=1, source_target_pairs={{0,1},{1,0},{2,3},{3,2},{4,5},{5,4},{6,7},{7,6},{8,9},{9,8},{10,11... | collective-permute-start | bytes 4915208 | tf_op jit(solution)/shard_map/ppermute | solution.py:538
  0.1 6.1 %copy-start.6 = (bf16[3200,2048]{1,0:T(8,128)(2,1)S(1)}, bf16[3200,2048]{1,0:T(8,128)(2,1)}, u32[]{:S(2)}) copy-start(bf16[3200,2048]{1,0:T(8,128)(2,1)} %w_ref.3) | copy-start | bytes 39321604
  4.4 1.9 %copy-start.7 = (bf16[4096]{0:T(1024)(128)(2,1)S(1)}, bf16[4096]{0:T(1024)(128)(2,1)}, u32[]{:S(2)}) copy-start(bf16[4096]{0:T(1024)(128)(2,1)} %rms_ref.1) | copy-start | bytes 24580
  4.4 1.9 %copy-start.8 = (bf16[2048]{0:T(1024)(128)(2,1)S(1)}, bf16[2048]{0:T(1024)(128)(2,1)}, u32[]{:S(2)}) copy-start(bf16[2048]{0:T(1024)(128)(2,1)} %add_ref.1) | copy-start | bytes 12292
  4.4 8.7 %slice-start = ((s8[12582912]{0:T(1024)(128)(4,1)}), s8[4194304]{0:T(1024)(128)(4,1)S(1)}, s32[]{:S(2)}) async-start(s8[12582912]{0:T(1024)(128)(4,1)} %bitcast.1), calls=%async_computation.1 | async-start | bytes 8388608
  6.2 6.9 %slice-start.1 = ((s8[12582912]{0:T(1024)(128)(4,1)}), s8[4194304]{0:T(1024)(128)(4,1)S(1)}, s32[]{:S(2)}) async-start(s8[12582912]{0:T(1024)(128)(4,1)} %bitcast.1), calls=%async_computation.2 | async-start | bytes 8388608
  6.3 6.9 %slice-start.2 = ((s8[12582912]{0:T(1024)(128)(4,1)}), s8[4194304]{0:T(1024)(128)(4,1)S(1)}, s32[]{:S(2)}) async-start(s8[12582912]{0:T(1024)(128)(4,1)} %bitcast.1), calls=%async_computation.3 | async-start | bytes 8388608
  12.5 4.6 %copy-start = (f32[512,128]{1,0:T(8,128)S(1)}, f32[512,128]{1,0:T(8,128)}, u32[]{:S(2)}) copy-start(f32[512,128]{1,0:T(8,128)} %constant.5.clone.sine_ref) | copy-start | bytes 786436
  12.5 4.6 %copy-start.1 = (f32[512,128]{1,0:T(8,128)S(1)}, f32[512,128]{1,0:T(8,128)}, u32[]{:S(2)}) copy-start(f32[512,128]{1,0:T(8,128)} %constant.4.clone.cos_ref) | copy-start | bytes 786436
  12.5 4.5 %collective-permute-start.1 = (bf16[512,2176]{1,0:T(8,128)(2,1)S(1)}, bf16[512,2176]{1,0:T(8,128)(2,1)S(1)}, u32[]{:S(2)}, u32[]{:S(2)}) collective-permute-start(bf16[512,2176]{1,0:T(8,128)(2,1)S(1)} %project.1.gained_ref.near_ref), channel_id=1, source_target_pairs={{0,1},{1,0},{2,3},{3,2},{4,5},{5,4},{6,7},{7,6},{8,9},{9,8},{10,11... | collective-permute-start | bytes 6684680 | tf_op jit(solution)/shard_map/ppermute | solution.py:544
